TPU v7x, 512 devices: a whole 4x8x8 slice. The times are simulated.
512 devices in a mesh: gz: 32 (over z, x_lo, core), grp: 16 (over y, x_hi).
Axes of the slice: x: 4 (x_hi: 2, x_lo: 2; x = x_hi * 2 + x_lo), y: 8, z: 8, core: 2. Of those that a mesh axis runs over, the one named last changes fastest.
Arguments:
- volumes: bfloat16 [16, 64, 16, 1024], P('grp', 'gz'), may hold values from -6 to 6
- cotangent: bfloat16 [16, 32, 64, 128], P(None, 'gz', None, 'grp'), may hold values from -6 to 6
- fine_kernel: bfloat16 [1728, 64], replicated, may hold values from -0.15625 to 0.15625
- down_kernel: bfloat16 [512, 128], replicated, may hold values from -0.25 to 0.25
- coarse_kernel: bfloat16 [3456, 128], P(None, 'grp'), may hold values from -0.109375 to 0.109375
Outputs:
- coarse_out: bfloat16 [16, 32, 64, 128], P(None, 'gz', None, 'grp')
- volume_grad: bfloat16 [16, 64, 16, 1024], P('grp', 'gz')
- fine_kernel_grad: float32 [1728, 64], replicated
- down_kernel_grad: float32 [512, 128], replicated
- coarse_kernel_grad: float32 [3456, 128], P(None, 'grp')
All inputs are finite; a program needn't handle non-finite values.
Results may differ from a plain program's by a relative error of at most 0.019.
Values may be sent and summed in bfloat16 or wider, within the bound.
No kernel may reach another device: no remote copies, remote signals or barrier semaphores. Data moves between devices by JAX's collectives and lax.ppermute only.
A program may use at most 64 MiB of HBM per device.

v0:
```python
import jax
import jax.numpy as jnp
from jax import lax
from jax.experimental import pallas as pl
from jax.experimental.pallas import tpu as pltpu
from jax.sharding import PartitionSpec as P


F32 = jnp.float32
BF16 = jnp.bfloat16
NN = (((1,), (0,)), ((), ()))
NT = (((1,), (1,)), ((), ()))
TN = (((0,), (0,)), ((), ()))


def mm(left, right, dims):
    return lax.dot_general(left, right, dims, preferred_element_type=F32)


def shift_rows(value, by, period):
    total = value.shape[0]
    place = lax.broadcasted_iota(jnp.int32, value.shape, 0) % period
    inside = place != (0 if by == 1 else period - 1)
    return jnp.where(inside, pltpu.roll(value, by % total, 0), 0.0)


def low_half(rows):
    return lax.broadcasted_iota(jnp.int32, (rows, 128), 1) < 64


def slope_and_silu(pre):
    sig = jax.nn.sigmoid(pre)
    return sig * (1.0 + pre * (1.0 - sig)), pre * sig


def fill_windows(windows, plane, blocks):
    low = low_half(16)
    none = jnp.zeros((16, 128), BF16)
    for j in range(8):
        after = blocks[j + 1] if j < 7 else none
        before = blocks[j - 1] if j > 0 else none
        rows = pl.ds(j * 16, 16)
        windows[plane, rows, 0:128] = blocks[j]
        windows[plane, rows, 128:256] = jnp.where(low, after, before)


def window_conv(windows, weights, dims):
    parts = []
    for dx in range(3):
        total = None
        for dz in range(3):
            rows = windows[dz : dz + 2].reshape(256, 256)
            term = mm(rows, weights[dz * 3 + dx], dims)
            total = term if total is None else total + term
        parts.append(total)
    return parts[1] + shift_rows(parts[0], 1, 16) + shift_rows(parts[2], -1, 16)


def place_weights(kernel, ahead, behind):
    low = low_half(64)
    tiles = [kernel[:, m * 128 : (m + 1) * 128].astype(F32) for m in range(13)]
    last = kernel[:, 1664:1728].astype(F32)
    tiles.append(jnp.concatenate([last, jnp.zeros((64, 64), F32)], axis=1))
    for k in range(9):
        first, second = tiles[3 * k // 2], tiles[3 * k // 2 + 1]
        swapped = pltpu.roll(jnp.where(low, second, first), 64, 1)
        if k % 2 == 0:
            zero_one, two_none = first, jnp.where(low, second, 0.0)
            one_two, none_zero = swapped, pltpu.roll(jnp.where(low, first, 0.0), 64, 1)
        else:
            one_two, none_zero = second, jnp.where(low, 0.0, first)
            zero_one, two_none = swapped, pltpu.roll(jnp.where(low, 0.0, second), 64, 1)
        blocks = [part.astype(BF16) for part in (one_two, zero_one, none_zero, two_none)]
        ahead[k, 0:64, 0:128] = blocks[0]
        ahead[k, 64:128, 0:128] = blocks[1]
        ahead[k, 0:64, 128:256] = blocks[2]
        ahead[k, 64:128, 128:256] = blocks[3]
        for slot in range(4):
            behind[8 - k, slot * 64 : (slot + 1) * 64] = blocks[slot]


def fine_forward(vol, before, after, weights, down, coarse, slope, windows, pooled, act):
    def lanes(ref, j):
        return ref[:, j * 128 : (j + 1) * 128]

    fill_windows(windows, 0, [lanes(before, j) for j in range(8)])
    fill_windows(windows, 1, [vol[0, :, j * 128 : (j + 1) * 128] for j in range(8)])
    fill_windows(windows, 2, [vol[1, :, j * 128 : (j + 1) * 128] for j in range(8)])
    fill_windows(windows, 3, [lanes(after, j) for j in range(8)])
    pre = window_conv(windows, weights, NT)
    slopes, silu = slope_and_silu(pre)
    slope[...] = slopes
    act[...] = silu
    for z in range(2):
        for bx in range(2):
            part = act[pl.ds(z * 128 + bx, 64, stride=2), :]
            at = (z * 2 + bx) * 128
            pooled[:, at : at + 128] = part.astype(BF16)
    coarse[...] = mm(pooled[...], down[...], NN).astype(BF16)


def y_taps(plane):
    value = plane[...].astype(F32)
    edge = jnp.zeros((8, 128), F32)
    earlier = jnp.concatenate([edge, value[:-8]], axis=0)
    later = jnp.concatenate([value[8:], edge], axis=0)
    return jnp.concatenate([earlier, value, later], axis=1).astype(BF16)


HALF = 1792


def spread_half(core, kernel, cotangent, out):
    for at in range(16):
        tail = jnp.concatenate([cotangent[at].astype(F32), jnp.zeros((8, 64), F32)], axis=1)
        out[at, :, HALF : HALF + 128] = tail.astype(BF16)

    @pl.when(core[0] == 0)
    def _():
        for at in range(16):
            out[at, :, 0:HALF] = kernel[:, 0:HALF]

    @pl.when(core[0] == 1)
    def _():
        for at in range(16):
            out[at, :, 0:HALF] = kernel[:, 3456 - HALF : 3456]


def coarse_forward(core, own, before, after, mine, other, grad, out, packed, scratch):
    rest = 3456 - HALF

    @pl.when(core[0] == 0)
    def _():
        packed[:, 0:HALF] = mine[:, 0:HALF]
        packed[:, HALF:3456] = other[:, HALF - rest : HALF]

    @pl.when(core[0] == 1)
    def _():
        packed[:, 0:rest] = other[:, 0:rest]
        packed[:, rest:3456] = mine[:, 0:HALF]

    planes = [y_taps(before), y_taps(own), y_taps(after)]
    parts = []
    for dx in range(3):
        total = None
        for dz in range(3):
            at = (dz * 3 + dx) * 384
            term = mm(planes[dz], packed[:, at : at + 384], NT)
            total = term if total is None else total + term
        parts.append(total)
    pre = parts[1] + shift_rows(parts[0], 1, 8) + shift_rows(parts[2], -1, 8)
    slopes, silu = slope_and_silu(pre)
    scratch[0:64] = silu
    by_x = [scratch[pl.ds(x, 8, stride=8), :] for x in range(8)]
    scratch[...] = mine[:, HALF : HALF + 128].astype(F32).T
    cotangent = jnp.concatenate([scratch[pl.ds(y, 8, stride=8), :] for y in range(8)], axis=0)
    slopes = (cotangent * slopes).astype(BF16)
    grad[...] = slopes
    out[...] = jnp.concatenate(by_x + [slopes.astype(F32)], axis=0).T.astype(BF16)


def coarse_kernel_terms(parts, features, terms, grads, taps):
    low = low_half(8)
    place = lax.broadcasted_iota(jnp.int32, (8, 128), 1) % 8
    for volume in range(16):
        taps[volume * 64 : (volume + 1) * 64] = y_taps(parts[volume, 0:64])
        features[volume] = parts[volume, 64:72, 0:64]
    for pair in range(8):
        first = parts[pair * 2, 64:80].astype(F32)
        second = parts[pair * 2 + 1, 64:80].astype(F32)
        own = jnp.where(low, pltpu.roll(first[0:8], 64, 1), second[0:8])
        before = jnp.where(low, first[8:16], pltpu.roll(second[8:16], 64, 1))
        after = jnp.where(low, pltpu.roll(first[8:16], 64, 1), second[8:16])
        for dz, value in enumerate((after, own, before)):
            earlier = jnp.where(place != 7, pltpu.roll(value, 127, 1), 0.0)
            later = jnp.where(place != 0, pltpu.roll(value, 1, 1), 0.0)
            for dx, moved in enumerate((earlier, value, later)):
                at = (dz * 3 + dx) * 8
                grads[at : at + 8, pair * 128 : (pair + 1) * 128] = moved
    total = mm(grads[...].astype(BF16), taps[...], NN)
    shared = []
    for at in range(80, 160, 16):
        both = jnp.sum(parts[:, at : at + 16, :].astype(F32), axis=0)
        shared += [both[0:8], both[8:16]]
    shared.append(jnp.sum(parts[:, 160:168, :].astype(F32), axis=0))
    none = jnp.zeros((8, 128), F32)
    for device in range(32):
        k, dy = divmod(device, 3)
        own = total[k * 8 : k * 8 + 8, dy * 128 : (dy + 1) * 128] if device < 27 else none
        other = shared[device] if device < 11 else none
        terms[device] = jnp.concatenate([own, other], axis=0).astype(BF16)


def backward(
    own, before, after, packed, pooled, slope, windows, down, coarse_in, features,
    out, fine_grad, act, shared,
):
    planes = [after[...], own[...], before[...]]
    edge = jnp.zeros((8, 128), F32)
    parts = []
    for dx in range(3):
        total = None
        for dz in range(3):
            at = (dz * 3 + dx) * 384
            term = mm(planes[dz], packed[:, at : at + 384], NN)
            total = term if total is None else total + term
        earlier = jnp.concatenate([total[8:, 0:128], edge], axis=0)
        later = jnp.concatenate([edge, total[:-8, 256:384]], axis=0)
        parts.append(earlier + total[:, 128:256] + later)
    in_grad = parts[1] + shift_rows(parts[0], -1, 8) + shift_rows(parts[2], 1, 8)
    in_grad = in_grad.astype(BF16)
    act_grad = mm(in_grad, down[...], NT)
    for z in range(2):
        for bx in range(2):
            at = (z * 2 + bx) * 128
            act[pl.ds(z * 128 + bx, 64, stride=2), :] = act_grad[:, at : at + 128]
    grad = (act[...] * slope[...]).astype(BF16)
    fine_grad[0] = grad[0:128]
    fine_grad[1] = grad[128:256]
    value = grad.astype(F32)
    moved = [shift_rows(value, -1, 16), value, shift_rows(value, 1, 16)]
    moved = [part.astype(BF16) for part in moved]
    low = low_half(64)
    held = None
    for dz in range(3):
        rows = windows[dz : dz + 2].reshape(256, 256)
        for dx in range(3):
            block = mm(moved[dx], rows, TN)
            u0, u1 = block[0:64, 0:128], block[0:64, 128:256]
            v0, v1 = block[64:128, 0:128], block[64:128, 128:256]
            for dy, (left, right) in enumerate(((u1, v0), (v0, u0), (u0, v1))):
                tap = (dz * 3 + dx) * 3 + dy
                if tap % 2 == 0:
                    held = pltpu.roll(left, 64, 1) + right
                else:
                    high = left + pltpu.roll(right, 64, 1)
                    at = (tap // 2) * 64
                    shared[at : at + 64] = jnp.where(low, held, high)
    shared[832:896] = jnp.where(low, held, 0.0)
    shared[896:1408] = mm(pooled[...], in_grad, TN)
    sides = jnp.concatenate([before[...].astype(F32), after[...].astype(F32)], axis=0).T
    for at in range(16):
        rows = slice(at * 8, at * 8 + 8)
        out[at, 0:64] = coarse_in[...]
        mixed = jnp.concatenate([features[rows].astype(F32), sides[rows]], axis=0)
        out[at, 64:80] = mixed.astype(BF16)
        out[at, 80:168] = shared[at * 88 : at * 88 + 88].astype(BF16)


def fine_backward(grad, before, after, weights, out, windows):
    def blocks(plane):
        return [plane[j * 16 : (j + 1) * 16] for j in range(8)]

    fill_windows(windows, 0, blocks(before[...]))
    fill_windows(windows, 1, blocks(grad[0]))
    fill_windows(windows, 2, blocks(grad[1]))
    fill_windows(windows, 3, blocks(after[...]))
    total = window_conv(windows, weights, NN).astype(BF16)
    for z in range(2):
        for j in range(8):
            at = z * 128 + j * 16
            out[z, :, j * 128 : (j + 1) * 128] = total[at : at + 16]


def sum_slabs(terms, out):
    total = jnp.sum(terms[...].astype(F32), axis=0).astype(BF16)
    for device in range(32):
        out[device] = total


def collect(terms, coarse, out):
    rows = []
    for device in range(27):
        both = terms[device].astype(F32)
        coarse[:, device * 128 : (device + 1) * 128] = both[0:8]
        rows.append(both[8:16])
    total = jnp.concatenate(rows[0:11], axis=0).astype(BF16)
    for device in range(16):
        out[device] = total


def unpack(shared, fine, down):
    for tile in range(13):
        rows = shared[tile * 64 : (tile + 1) * 64]
        fine[:, tile * 128 : (tile + 1) * 128] = rows.astype(F32)
    fine[:, 1664:1728] = shared[832:896].astype(F32)[:, 0:64]
    down[...] = shared[896:1408].astype(F32)


def call(body, outs, *operands, scratch=(), far=(), core=None, moved=True):
    place = [jax.ShapeDtypeStruct if at in far else pltpu.VMEM for at in range(len(outs))]
    first = [] if core is None else [core]
    if moved:
        operands = [pltpu.with_memory_space_constraint(part, pltpu.VMEM) for part in operands]
    specs = [pl.BlockSpec(memory_space=pltpu.SMEM) for _ in first]
    return pl.pallas_call(
        body,
        out_shape=[put(*out) for put, out in zip(place, outs)],
        in_specs=specs + [pl.BlockSpec(memory_space=pltpu.VMEM) for _ in operands],
        scratch_shapes=[pltpu.VMEM(shape, kind) for shape, kind in scratch],
        cost_estimate=pl.CostEstimate(flops=WORK, transcendentals=0, bytes_accessed=1 << 20),
        interpret=INTERPRET,
    )(*first, *operands)


INTERPRET = False
WORK = 250_000_000


def from_sides(last, first):
    devices = lax.axis_size("gz")
    up = [(i, i + 1) for i in range(devices - 1)]
    down = [(j, i) for i, j in up]
    return lax.ppermute(last, "gz", up), lax.ppermute(first, "gz", down)


def exchange(blocks, axis):
    return lax.all_to_all(blocks, axis, 0, 0, tiled=True)


def per_device(volumes, cotangent, fine_kernel, down_kernel, coarse_kernel):
    group = lax.axis_size("grp")
    slabs = lax.axis_size("gz")
    vol = volumes[0]
    before, after = from_sides(vol[1], vol[0])
    core = (lax.axis_index("gz") & 1).astype(jnp.int32).reshape(1)
    (halves,) = call(
        spread_half,
        [((group, 8, HALF + 128), BF16)],
        coarse_kernel.T, jnp.swapaxes(cotangent[:, 0], 1, 2),
        core=core,
        moved=False,
    )
    mine = exchange(halves, "grp").reshape(128, HALF + 128)
    ahead, behind = call(
        place_weights, [((9, 128, 256), BF16), ((9, 256, 128), BF16)], fine_kernel.T, far=(1,)
    )

    coarse_in, slope, windows, pooled = call(
        fine_forward,
        [((64, 128), BF16), ((256, 128), F32), ((4, 128, 256), BF16), ((64, 512), BF16)],
        vol, before, after, ahead, down_kernel,
        scratch=[((256, 128), F32)],
        far=(2,),
    )
    in_before, in_after = from_sides(coarse_in, coarse_in)
    mine, slope = lax.optimization_barrier((mine, slope))
    other = lax.ppermute(mine, "gz", [(i, i ^ 1) for i in range(slabs)])
    coarse_grad, features, packed = call(
        coarse_forward,
        [((64, 128), BF16), ((128, 128), BF16), ((128, 3456), BF16)],
        coarse_in, in_before, in_after, mine, other,
        scratch=[((128, 128), F32)],
        core=core,
    )
    grad_before, grad_after = from_sides(coarse_grad, coarse_grad)
    parts, fine_grad = call(
        backward,
        [((group, 168, 128), BF16), ((2, 128, 128), BF16)],
        coarse_grad, grad_before, grad_after, packed, pooled, slope, windows, down_kernel,
        coarse_in, features,
        scratch=[((256, 128), F32), ((1408, 128), F32)],
    )
    parts = exchange(parts, "grp")
    fine_before, fine_after = from_sides(fine_grad[1], fine_grad[0])
    (volume_grad,) = call(
        fine_backward,
        [((2, 16, 1024), BF16)],
        fine_grad, fine_before, fine_after, behind,
        scratch=[((4, 128, 256), BF16)],
        far=(0,),
    )
    parts, volume_grad = lax.optimization_barrier((parts, volume_grad))
    out_rows, terms = call(
        coarse_kernel_terms,
        [((group, 8, 64), BF16), ((slabs, 16, 128), BF16)],
        parts,
        scratch=[((72, 1024), F32), ((1024, 384), BF16)],
        far=(0,),
    )
    terms = exchange(terms, "gz")
    (terms,) = call(sum_slabs, [((slabs, 16, 128), BF16)], terms)
    terms = exchange(terms, "gz")
    coarse_kg, shared = call(collect, [((8, 3456), F32), ((group, 88, 128), BF16)], terms, far=(0,))
    shared = exchange(shared, "grp").reshape(1408, 128)
    fine_kg, down_kg = call(unpack, [((64, 1728), F32), ((512, 128), F32)], shared, far=(0, 1))
    coarse_out = jnp.swapaxes(out_rows, 1, 2)[:, None]
    return (coarse_out, volume_grad[None], fine_kg.T, down_kg, coarse_kg.T)


def solution(mesh):
    in_specs = (P("grp", "gz", None, None), P(None, "gz", None, "grp"), P(), P(), P(None, "grp"))
    out_specs = (P(None, "gz", None, "grp"), P("grp", "gz", None, None), P(), P(), P(None, "grp"))
    return jax.shard_map(
        per_device, mesh=mesh, in_specs=in_specs, out_specs=out_specs, check_vma=False
    )
```

profile of v0, /device:TPU:1, one launch (start us, length us, event | category | flops | bytes accessed | tf_op | source)
XLA Modules:
  0.0 130.5 jit_solution(5901587931756796844)
XLA Ops:
  0.6 1.7 %shard_map.94 = bf16[16,8,1920]{2,1,0:T(8,128)(2,1)} custom-call(s32[1]{0:T(128)} %bitcast.core, bf16[8,3456]{1,0:T(8,128)(2,1)} %bitcast.30, bf16[16,8,64]{2,1,0:T(8,128)(2,1)} %bitcast.31), custom_call_target="tpu_custom_call" | custom-call | flops 250000000 | bytes 1048576 | tf_op jit(solution)/shard_map/pallas_call | solution.py:296
  2.3 10.3 %all-to-all-start = ((bf16[16,8,1920]{2,1,0:T(8,128)(2,1)}), bf16[16,8,1920]{2,1,0:T(8,128)(2,1)S(1)}, u32[]{:S(2)}, u32[]{:S(2)}) async-start(bf16[16,8,1920]{2,1,0:T(8,128)(2,1)} %shard_map.94), calls=%async_computation | async-start | bytes 983040 | tf_op jit(solution)/shard_map/all_to_all | solution.py:318
  12.7 2.9 %collective-permute-start.1 = (bf16[16,1024]{1,0:T(8,128)(2,1)S(1)}, bf16[16,1024]{1,0:T(8,128)(2,1)S(1)}, u32[]{:S(2)}, u32[]{:S(2)}) collective-permute-start(bf16[16,1024]{1,0:T(8,128)(2,1)S(1)} %get-tuple-element.54), channel_id=1, source_target_pairs={{16,0},{32,16},{48,32},{64,48},{80,64},{96,80},{112,96},{128,112},... | collective-permute-start | bytes 98312 | tf_op jit(solution)/shard_map/ppermute | solution.py:314
  15.5 2.7 %collective-permute-start = (bf16[16,1024]{1,0:T(8,128)(2,1)S(1)}, bf16[16,1024]{1,0:T(8,128)(2,1)S(1)}, u32[]{:S(2)}, u32[]{:S(2)}) collective-permute-start(bf16[16,1024]{1,0:T(8,128)(2,1)S(1)} %get-tuple-element.55), channel_id=1, source_target_pairs={{0,16},{16,32},{32,48},{48,64},{64,80},{80,96},{96,112},{112,128},... | collective-permute-start | bytes 98312 | tf_op jit(solution)/shard_map/ppermute | solution.py:314
  18.3 0.0 copy-start.1
  18.3 1.0 shard_map.92
  19.2 0.0 collective-permute-done.1.after
  19.3 0.0 collective-permute-done.before
  19.3 0.8 shard_map.93
  20.1 9.1 %all-to-all-done = bf16[16,8,1920]{2,1,0:T(8,128)(2,1)S(1)} async-done(((bf16[16,8,1920]{2,1,0:T(8,128)(2,1)}), bf16[16,8,1920]{2,1,0:T(8,128)(2,1)S(1)}, u32[]{:S(2)}, u32[]{:S(2)}) %all-to-all-start) | async-done | bytes 491552 | tf_op jit(solution)/shard_map/all_to_all | solution.py:318
  29.2 4.2 %collective-permute-start.4 = (bf16[128,1920]{1,0:T(8,128)(2,1)S(1)}, bf16[128,1920]{1,0:T(8,128)(2,1)S(1)}, u32[]{:S(2)}, u32[]{:S(2)}) collective-permute-start(bf16[128,1920]{1,0:T(8,128)(2,1)S(1)} %bitcast.25), channel_id=1, source_target_pairs={{0,16},{16,0},{32,48},{48,32},{64,80},{80,64},{96,112},{112,96},{1... | collective-permute-start | bytes 1474568 | tf_op jit(solution)/shard_map/ppermute | solution.py:348
  33.5 0.0 copy-start
  33.5 2.1 %collective-permute-start.3 = (bf16[64,128]{1,0:T(8,128)(2,1)S(1)}, bf16[64,128]{1,0:T(8,128)(2,1)S(1)}, u32[]{:S(2)}, u32[]{:S(2)}) collective-permute-start(bf16[64,128]{1,0:T(8,128)(2,1)S(1)} %get-tuple-element.27.own.coarse_in), channel_id=1, source_target_pairs={{16,0},{32,16},{48,32},{64,48},{80,64},{96,80},{112,96},{128,112},... | collective-permute-start | bytes 49160 | tf_op jit(solution)/shard_map/ppermute | solution.py:314
  35.5 3.6 %collective-permute-start.2 = (bf16[64,128]{1,0:T(8,128)(2,1)S(1)}, bf16[64,128]{1,0:T(8,128)(2,1)S(1)}, u32[]{:S(2)}, u32[]{:S(2)}) collective-permute-start(bf16[64,128]{1,0:T(8,128)(2,1)S(1)} %get-tuple-element.27.own.coarse_in), channel_id=1, source_target_pairs={{0,16},{16,32},{32,48},{48,64},{64,80},{80,96},{96,112},{112,128},... | collective-permute-start | bytes 49160 | tf_op jit(solution)/shard_map/ppermute | solution.py:314
  39.2 0.8 collective-permute-done.2.before
  40.0 0.7 shard_map.95
  40.7 1.9 %collective-permute-start.6 = (bf16[64,128]{1,0:T(8,128)(2,1)S(1)}, bf16[64,128]{1,0:T(8,128)(2,1)S(1)}, u32[]{:S(2)}, u32[]{:S(2)}) collective-permute-start(bf16[64,128]{1,0:T(8,128)(2,1)S(1)} %get-tuple-element.30.own), channel_id=1, source_target_pairs={{16,0},{32,16},{48,32},{64,48},{80,64},{96,80},{112,96},{128,112},... | collective-permute-start | bytes 49160 | tf_op jit(solution)/shard_map/ppermute | solution.py:314
  42.7 4.2 %collective-permute-start.5 = (bf16[64,128]{1,0:T(8,128)(2,1)S(1)}, bf16[64,128]{1,0:T(8,128)(2,1)S(1)}, u32[]{:S(2)}, u32[]{:S(2)}) collective-permute-start(bf16[64,128]{1,0:T(8,128)(2,1)S(1)} %get-tuple-element.30.own), channel_id=1, source_target_pairs={{0,16},{16,32},{32,48},{48,64},{64,80},{80,96},{96,112},{112,128},... | collective-permute-start | bytes 49160 | tf_op jit(solution)/shard_map/ppermute | solution.py:314
  46.9 0.8 collective-permute-done.5.before
  47.7 1.8 %shard_map.96 = (bf16[16,168,128]{2,1,0:T(8,128)(2,1)}, bf16[2,128,128]{2,1,0:T(8,128)(2,1)S(1)}) custom-call(bf16[64,128]{1,0:T(8,128)(2,1)S(1)} %get-tuple-element.30.own, bf16[64,128]{1,0:T(8,128)(2,1)S(1)} %collective-permute-done.5.before, bf16[64,128]{1,0:T(8,128)(2,1)S(1)} %collective-permute-done.6.after, ...), custom_call_target="tpu_custom_call" | custom-call | flops 250000000 | bytes 1048576 | tf_op jit(solution)/shard_map/pallas_call | solution.py:296
  49.5 3.7 %all-to-all-start.1 = ((bf16[16,168,128]{2,1,0:T(8,128)(2,1)}), bf16[16,168,128]{2,1,0:T(8,128)(2,1)S(1)}, u32[]{:S(2)}, u32[]{:S(2)}) async-start(bf16[16,168,128]{2,1,0:T(8,128)(2,1)} %get-tuple-element.36), calls=%async_computation.1 | async-start | bytes 1376256 | tf_op jit(solution)/shard_map/all_to_all | solution.py:318
  53.2 1.9 %collective-permute-start.8 = (bf16[128,128]{1,0:T(8,128)(2,1)S(1)}, bf16[128,128]{1,0:T(8,128)(2,1)S(1)}, u32[]{:S(2)}, u32[]{:S(2)}) collective-permute-start(bf16[128,128]{1,0:T(8,128)(2,1)S(1)} %get-tuple-element.52), channel_id=1, source_target_pairs={{16,0},{32,16},{48,32},{64,48},{80,64},{96,80},{112,96},{128,112},... | collective-permute-start | bytes 98312 | tf_op jit(solution)/shard_map/ppermute | solution.py:314
  55.2 4.2 %collective-permute-start.7 = (bf16[128,128]{1,0:T(8,128)(2,1)S(1)}, bf16[128,128]{1,0:T(8,128)(2,1)S(1)}, u32[]{:S(2)}, u32[]{:S(2)}) collective-permute-start(bf16[128,128]{1,0:T(8,128)(2,1)S(1)} %get-tuple-element.53), channel_id=1, source_target_pairs={{0,16},{16,32},{32,48},{48,64},{64,80},{80,96},{96,112},{112,128},... | collective-permute-start | bytes 98312 | tf_op jit(solution)/shard_map/ppermute | solution.py:314
  59.4 1.0 collective-permute-done.7.before
  60.4 1.1 shard_map.97
  61.5 13.4 %all-to-all-done.1.parts = bf16[16,168,128]{2,1,0:T(8,128)(2,1)S(1)} async-done(((bf16[16,168,128]{2,1,0:T(8,128)(2,1)}), bf16[16,168,128]{2,1,0:T(8,128)(2,1)S(1)}, u32[]{:S(2)}, u32[]{:S(2)}) %all-to-all-start.1) | async-done | bytes 688160 | tf_op jit(solution)/shard_map/all_to_all | solution.py:318
  74.9 0.9 shard_map.98
  75.9 23.3 %all_to_all.25.terms = bf16[32,16,128]{2,1,0:T(8,128)(2,1)S(1)} all-to-all(bf16[32,16,128]{2,1,0:T(8,128)(2,1)S(1)} %get-tuple-element.42), channel_id=1, replica_groups=mesh['gz'=32,'grp'=16] {'gz'}, dimensions={0} | all-to-all | bytes 262144 | tf_op jit(solution)/shard_map/all_to_all | solution.py:318
  99.3 12.5 %all_to_all.26.terms = bf16[32,16,128]{2,1,0:T(8,128)(2,1)S(1)} all-to-all(bf16[32,16,128]{2,1,0:T(8,128)(2,1)S(1)} %shard_map.99), channel_id=1, replica_groups=mesh['gz'=32,'grp'=16] {'gz'}, dimensions={0} | all-to-all | bytes 262144 | tf_op jit(solution)/shard_map/all_to_all | solution.py:318
  111.8 0.7 shard_map.100
  112.5 17.1 %all_to_all.27 = bf16[16,88,128]{2,1,0:T(8,128)(2,1)S(1)} all-to-all(bf16[16,88,128]{2,1,0:T(8,128)(2,1)S(1)} %get-tuple-element.43), channel_id=1, replica_groups=mesh['gz'=32,'grp'=16] {'grp'}, dimensions={0} | all-to-all | bytes 720896 | tf_op jit(solution)/shard_map/all_to_all | solution.py:318
  129.6 0.9 shard_map.101
  (15 shorter events, 0.1 us)
Async XLA Ops:
  2.3 10.3 %copy-start.2 = (bf16[1,2,16,1024]{3,2,1,0:T(8,128)(2,1)S(1)}, bf16[1,2,16,1024]{3,2,1,0:T(8,128)(2,1)}, u32[]{:S(2)}) copy-start(bf16[1,2,16,1024]{3,2,1,0:T(8,128)(2,1)} %param.5) | copy-start | bytes 196612
  2.3 15.9 %copy-start.3 = (bf16[1728,64]{0,1:T(8,128)(2,1)S(1)}, bf16[1728,64]{0,1:T(8,128)(2,1)}, u32[]{:S(2)}) copy-start(bf16[1728,64]{0,1:T(8,128)(2,1)} %param.7) | copy-start | bytes 663556
  2.3 26.9 %all-to-all-start = ((bf16[16,8,1920]{2,1,0:T(8,128)(2,1)}), bf16[16,8,1920]{2,1,0:T(8,128)(2,1)S(1)}, u32[]{:S(2)}, u32[]{:S(2)}) async-start(bf16[16,8,1920]{2,1,0:T(8,128)(2,1)} %shard_map.94), calls=%async_computation | async-start | bytes 983040 | tf_op jit(solution)/shard_map/all_to_all | solution.py:318
  12.7 6.6 %collective-permute-start.1 = (bf16[16,1024]{1,0:T(8,128)(2,1)S(1)}, bf16[16,1024]{1,0:T(8,128)(2,1)S(1)}, u32[]{:S(2)}, u32[]{:S(2)}) collective-permute-start(bf16[16,1024]{1,0:T(8,128)(2,1)S(1)} %get-tuple-element.54), channel_id=1, source_target_pairs={{16,0},{32,16},{48,32},{64,48},{80,64},{96,80},{112,96},{128,112},... | collective-permute-start | bytes 98312 | tf_op jit(solution)/shard_map/ppermute | solution.py:314
  15.5 3.7 %collective-permute-start = (bf16[16,1024]{1,0:T(8,128)(2,1)S(1)}, bf16[16,1024]{1,0:T(8,128)(2,1)S(1)}, u32[]{:S(2)}, u32[]{:S(2)}) collective-permute-start(bf16[16,1024]{1,0:T(8,128)(2,1)S(1)} %get-tuple-element.55), channel_id=1, source_target_pairs={{0,16},{16,32},{32,48},{48,64},{64,80},{80,96},{96,112},{112,128},... | collective-permute-start | bytes 98312 | tf_op jit(solution)/shard_map/ppermute | solution.py:314
  18.3 1.0 copy-start.1
  29.2 10.8 %collective-permute-start.4 = (bf16[128,1920]{1,0:T(8,128)(2,1)S(1)}, bf16[128,1920]{1,0:T(8,128)(2,1)S(1)}, u32[]{:S(2)}, u32[]{:S(2)}) collective-permute-start(bf16[128,1920]{1,0:T(8,128)(2,1)S(1)} %bitcast.25), channel_id=1, source_target_pairs={{0,16},{16,0},{32,48},{48,32},{64,80},{80,64},{96,112},{112,96},{1... | collective-permute-start | bytes 1474568 | tf_op jit(solution)/shard_map/ppermute | solution.py:348
  33.5 14.3 %copy-start = (bf16[4,128,256]{2,1,0:T(8,128)(2,1)S(1)}, bf16[4,128,256]{2,1,0:T(8,128)(2,1)}, u32[]{:S(2)}) copy-start(bf16[4,128,256]{2,1,0:T(8,128)(2,1)} %get-tuple-element.34.windows) | copy-start | bytes 786436
  33.5 5.7 %collective-permute-start.3 = (bf16[64,128]{1,0:T(8,128)(2,1)S(1)}, bf16[64,128]{1,0:T(8,128)(2,1)S(1)}, u32[]{:S(2)}, u32[]{:S(2)}) collective-permute-start(bf16[64,128]{1,0:T(8,128)(2,1)S(1)} %get-tuple-element.27.own.coarse_in), channel_id=1, source_target_pairs={{16,0},{32,16},{48,32},{64,48},{80,64},{96,80},{112,96},{128,112},... | collective-permute-start | bytes 49160 | tf_op jit(solution)/shard_map/ppermute | solution.py:314
  35.5 4.5 %collective-permute-start.2 = (bf16[64,128]{1,0:T(8,128)(2,1)S(1)}, bf16[64,128]{1,0:T(8,128)(2,1)S(1)}, u32[]{:S(2)}, u32[]{:S(2)}) collective-permute-start(bf16[64,128]{1,0:T(8,128)(2,1)S(1)} %get-tuple-element.27.own.coarse_in), channel_id=1, source_target_pairs={{0,16},{16,32},{32,48},{48,64},{64,80},{80,96},{96,112},{112,128},... | collective-permute-start | bytes 49160 | tf_op jit(solution)/shard_map/ppermute | solution.py:314
  40.7 6.1 %collective-permute-start.6 = (bf16[64,128]{1,0:T(8,128)(2,1)S(1)}, bf16[64,128]{1,0:T(8,128)(2,1)S(1)}, u32[]{:S(2)}, u32[]{:S(2)}) collective-permute-start(bf16[64,128]{1,0:T(8,128)(2,1)S(1)} %get-tuple-element.30.own), channel_id=1, source_target_pairs={{16,0},{32,16},{48,32},{64,48},{80,64},{96,80},{112,96},{128,112},... | collective-permute-start | bytes 49160 | tf_op jit(solution)/shard_map/ppermute | solution.py:314
  42.7 5.1 %collective-permute-start.5 = (bf16[64,128]{1,0:T(8,128)(2,1)S(1)}, bf16[64,128]{1,0:T(8,128)(2,1)S(1)}, u32[]{:S(2)}, u32[]{:S(2)}) collective-permute-start(bf16[64,128]{1,0:T(8,128)(2,1)S(1)} %get-tuple-element.30.own), channel_id=1, source_target_pairs={{0,16},{16,32},{32,48},{48,64},{64,80},{80,96},{96,112},{112,128},... | collective-permute-start | bytes 49160 | tf_op jit(solution)/shard_map/ppermute | solution.py:314
  49.5 10.9 %copy-start.4 = (bf16[9,256,128]{2,1,0:T(8,128)(2,1)S(1)}, bf16[9,256,128]{2,1,0:T(8,128)(2,1)}, u32[]{:S(2)}) copy-start(bf16[9,256,128]{2,1,0:T(8,128)(2,1)} %get-tuple-element.38.weights) | copy-start | bytes 1769476
  49.5 25.4 %all-to-all-start.1 = ((bf16[16,168,128]{2,1,0:T(8,128)(2,1)}), bf16[16,168,128]{2,1,0:T(8,128)(2,1)S(1)}, u32[]{:S(2)}, u32[]{:S(2)}) async-start(bf16[16,168,128]{2,1,0:T(8,128)(2,1)} %get-tuple-element.36), calls=%async_computation.1 | async-start | bytes 1376256 | tf_op jit(solution)/shard_map/all_to_all | solution.py:318
  53.2 6.1 %collective-permute-start.8 = (bf16[128,128]{1,0:T(8,128)(2,1)S(1)}, bf16[128,128]{1,0:T(8,128)(2,1)S(1)}, u32[]{:S(2)}, u32[]{:S(2)}) collective-permute-start(bf16[128,128]{1,0:T(8,128)(2,1)S(1)} %get-tuple-element.52), channel_id=1, source_target_pairs={{16,0},{32,16},{48,32},{64,48},{80,64},{96,80},{112,96},{128,112},... | collective-permute-start | bytes 98312 | tf_op jit(solution)/shard_map/ppermute | solution.py:314
  55.2 5.2 %collective-permute-start.7 = (bf16[128,128]{1,0:T(8,128)(2,1)S(1)}, bf16[128,128]{1,0:T(8,128)(2,1)S(1)}, u32[]{:S(2)}, u32[]{:S(2)}) collective-permute-start(bf16[128,128]{1,0:T(8,128)(2,1)S(1)} %get-tuple-element.53), channel_id=1, source_target_pairs={{0,16},{16,32},{32,48},{48,64},{64,80},{80,96},{96,112},{112,128},... | collective-permute-start | bytes 98312 | tf_op jit(solution)/shard_map/ppermute | solution.py:314
where the time goes:
time: 131 us
  blocking collectives  53 us (40%)
  starting transfers between devices  41.8 us (32%)
  waiting for transfers between devices  25.2 us (19%)
  Pallas kernels  9.6 us (7%)
    all_to_all x3, blocking collectives, exchange(): return lax.all_to_all(blocks, axis, 0, 0, tiled=True)  53 us
    ppermute x8, starting transfers between devices, from_sides(): return (lax.ppermute(last, 'gz', up), lax.ppermute(first, 'gz', down))  23.5 us
    all_to_all x2, waiting for transfers between devices, exchange(): return lax.all_to_all(blocks, axis, 0, 0, tiled=True)  22.5 us
    all_to_all x2, starting transfers between devices, exchange(): return lax.all_to_all(blocks, axis, 0, 0, tiled=True)  14.1 us
    pallas_call x10, Pallas kernels, call(): pl.pallas_call(body, out_shape=[put(*out) for put, out in zip(place, outs...  9.6 us
    ppermute x1, starting transfers between devices, per_device(): other = lax.ppermute(mine, 'gz', [(i, i ^ 1) for i in range(slabs)])  4.23 us
    ppermute x8, waiting for transfers between devices, from_sides(): return (lax.ppermute(last, 'gz', up), lax.ppermute(first, 'gz', down))  2.71 us
  transfers between devices with their start and end apart: 11, of which 5 were waited for; matrix products, arithmetic and copies ran while one was open for 0% of the time, Pallas kernels for 2%

commit v1 on v0

--- a/solution.py
+++ b/solution.py
@@ -79,14 +79,30 @@
             behind[8 - k, slot * 64 : (slot + 1) * 64] = blocks[slot]
 
 
-def fine_forward(vol, before, after, weights, down, coarse, slope, windows, pooled, act):
-    def lanes(ref, j):
-        return ref[:, j * 128 : (j + 1) * 128]
-
-    fill_windows(windows, 0, [lanes(before, j) for j in range(8)])
+def sort_sides(core, near, far, sides):
+    @pl.when(core[0] == 0)
+    def _():
+        sides[0] = far[...]
+        sides[1] = near[...]
+
+    @pl.when(core[0] == 1)
+    def _():
+        sides[0] = near[...]
+        sides[1] = far[...]
+
+
+def fine_forward(
+    core, vol, near, far, weights, down, coarse, slope, windows, pooled, act, sides
+):
+    sort_sides(core, near, far, sides)
+
+    def lanes(side, j):
+        return sides[side, :, j * 128 : (j + 1) * 128]
+
+    fill_windows(windows, 0, [lanes(0, j) for j in range(8)])
     fill_windows(windows, 1, [vol[0, :, j * 128 : (j + 1) * 128] for j in range(8)])
     fill_windows(windows, 2, [vol[1, :, j * 128 : (j + 1) * 128] for j in range(8)])
-    fill_windows(windows, 3, [lanes(after, j) for j in range(8)])
+    fill_windows(windows, 3, [lanes(1, j) for j in range(8)])
     pre = window_conv(windows, weights, NT)
     slopes, silu = slope_and_silu(pre)
     slope[...] = slopes
@@ -126,7 +142,9 @@
             out[at, :, 0:HALF] = kernel[:, 3456 - HALF : 3456]
 
 
-def coarse_forward(core, own, before, after, mine, other, grad, out, packed, scratch):
+def coarse_forward(core, own, near, far, mine, other, grad, out, packed, scratch, sides):
+    sort_sides(core, near, far, sides)
+    before, after = sides.at[0], sides.at[1]
     rest = 3456 - HALF
 
     @pl.when(core[0] == 0)
@@ -192,9 +210,11 @@
 
 
 def backward(
-    own, before, after, packed, pooled, slope, windows, down, coarse_in, features,
-    out, fine_grad, act, shared,
+    core, own, near, far, packed, pooled, slope, windows, down, coarse_in, features,
+    out, fine_grad, act, shared, sides,
 ):
+    sort_sides(core, near, far, sides)
+    before, after = sides.at[0], sides.at[1]
     planes = [after[...], own[...], before[...]]
     edge = jnp.zeros((8, 128), F32)
     parts = []
@@ -314,6 +334,14 @@
     return lax.ppermute(last, "gz", up), lax.ppermute(first, "gz", down)
 
 
+def pair_swaps(to_core, to_other):
+    devices = lax.axis_size("gz")
+    up = [(i, i + 1) for i in range(1, devices - 1, 2)]
+    near = lax.ppermute(to_core, "gz", [(i, i ^ 1) for i in range(devices)])
+    far = lax.ppermute(to_other, "gz", up + [(j, i) for i, j in up])
+    return near, far
+
+
 def exchange(blocks, axis):
     return lax.all_to_all(blocks, axis, 0, 0, tiled=True)
 
@@ -322,7 +350,6 @@
     group = lax.axis_size("grp")
     slabs = lax.axis_size("gz")
     vol = volumes[0]
-    before, after = from_sides(vol[1], vol[0])
     core = (lax.axis_index("gz") & 1).astype(jnp.int32).reshape(1)
     (halves,) = call(
         spread_half,
@@ -331,6 +358,11 @@
         core=core,
         moved=False,
     )
+    index = core[0]
+    near, far = pair_swaps(
+        lax.dynamic_index_in_dim(vol, 1 - index, 0, keepdims=False),
+        lax.dynamic_index_in_dim(vol, index, 0, keepdims=False),
+    )
     mine = exchange(halves, "grp").reshape(128, HALF + 128)
     ahead, behind = call(
         place_weights, [((9, 128, 256), BF16), ((9, 256, 128), BF16)], fine_kernel.T, far=(1,)
@@ -339,27 +371,29 @@
     coarse_in, slope, windows, pooled = call(
         fine_forward,
         [((64, 128), BF16), ((256, 128), F32), ((4, 128, 256), BF16), ((64, 512), BF16)],
-        vol, before, after, ahead, down_kernel,
-        scratch=[((256, 128), F32)],
+        vol, near, far, ahead, down_kernel,
+        scratch=[((256, 128), F32), ((2, 16, 1024), BF16)],
+        core=core,
         far=(2,),
     )
-    in_before, in_after = from_sides(coarse_in, coarse_in)
+    in_near, in_far = pair_swaps(coarse_in, coarse_in)
     mine, slope = lax.optimization_barrier((mine, slope))
     other = lax.ppermute(mine, "gz", [(i, i ^ 1) for i in range(slabs)])
     coarse_grad, features, packed = call(
         coarse_forward,
         [((64, 128), BF16), ((128, 128), BF16), ((128, 3456), BF16)],
-        coarse_in, in_before, in_after, mine, other,
-        scratch=[((128, 128), F32)],
+        coarse_in, in_near, in_far, mine, other,
+        scratch=[((128, 128), F32), ((2, 64, 128), BF16)],
         core=core,
     )
-    grad_before, grad_after = from_sides(coarse_grad, coarse_grad)
+    grad_near, grad_far = pair_swaps(coarse_grad, coarse_grad)
     parts, fine_grad = call(
         backward,
         [((group, 168, 128), BF16), ((2, 128, 128), BF16)],
-        coarse_grad, grad_before, grad_after, packed, pooled, slope, windows, down_kernel,
+        coarse_grad, grad_near, grad_far, packed, pooled, slope, windows, down_kernel,
         coarse_in, features,
-        scratch=[((256, 128), F32), ((1408, 128), F32)],
+        scratch=[((256, 128), F32), ((1408, 128), F32), ((2, 64, 128), BF16)],
+        core=core,
     )
     parts = exchange(parts, "grp")
     fine_before, fine_after = from_sides(fine_grad[1], fine_grad[0])

time: 131 us -> 130 us (level)
  starting transfers between devices: 41.8 us -> 39.9 us
    ppermute x8 -> x2, starting transfers between devices: 23.5 us -> 5.56 us  [from_sides(): return (lax.ppermute(last, 'gz', up), lax.ppermute(first, 'gz', down))]
    ppermute x0 -> x6, starting transfers between devices: none -> 16 us  [the longest x3 10.2 us: pair_swaps(): far = lax.ppermute(to_other, 'gz', up + [(j, i) for i, j in up])]
    ppermute x0 -> x6, waiting for transfers between devices: none -> 2.45 us  [the longest x3 1.45 us: pair_swaps(): near = lax.ppermute(to_core, 'gz', [(i, i ^ 1) for i in range(devices)])]
    ppermute x8 -> x2, waiting for transfers between devices: 2.71 us -> 0.99 us  [from_sides(): return (lax.ppermute(last, 'gz', up), lax.ppermute(first, 'gz', down))]
  transfers between devices with their start and end apart: 11 -> 11, of which waited for: 5 -> 7; matrix products, arithmetic and copies ran while one was open for 0% -> 0% of each run, Pallas kernels for 2% -> 2%
where the time goes in v1:
time: 130 us; the launch traced here: 129 us
  blocking collectives  52.5 us (40%)
  starting transfers between devices  39.9 us (31%)
  waiting for transfers between devices  26 us (20%)
  Pallas kernels  9.57 us (7%)
    all_to_all x3, blocking collectives, exchange(): return lax.all_to_all(blocks, axis, 0, 0, tiled=True)  52.5 us
    all_to_all x2, waiting for transfers between devices, exchange(): return lax.all_to_all(blocks, axis, 0, 0, tiled=True)  22.6 us
    all_to_all x2, starting transfers between devices, exchange(): return lax.all_to_all(blocks, axis, 0, 0, tiled=True)  14.1 us
    ppermute x3, starting transfers between devices, pair_swaps(): far = lax.ppermute(to_other, 'gz', up + [(j, i) for i, j in up])  10.2 us
    pallas_call x10, Pallas kernels, call(): pl.pallas_call(body, out_shape=[put(*out) for put, out in zip(place, outs...  9.57 us
    ppermute x3, starting transfers between devices, pair_swaps(): near = lax.ppermute(to_core, 'gz', [(i, i ^ 1) for i in range(devices)])  5.76 us
    ppermute x2, starting transfers between devices, from_sides(): return (lax.ppermute(last, 'gz', up), lax.ppermute(first, 'gz', down))  5.56 us
    ppermute x1, starting transfers between devices, per_device(): other = lax.ppermute(mine, 'gz', [(i, i ^ 1) for i in range(slabs)])  4.23 us
  transfers between devices with their start and end apart: 11, of which 7 were waited for; matrix products, arithmetic and copies ran while one was open for 0% of the time, Pallas kernels for 2%

profile of v1, /device:TPU:1, one launch (start us, length us, event | category | flops | bytes accessed | tf_op | source)
XLA Modules:
  0.0 128.7 jit_solution(5525387835093880737)
XLA Ops:
  0.6 1.7 %shard_map.94 = bf16[16,8,1920]{2,1,0:T(8,128)(2,1)} custom-call(s32[1]{0:T(128)} %bitcast.core, bf16[8,3456]{1,0:T(8,128)(2,1)} %bitcast.30, bf16[16,8,64]{2,1,0:T(8,128)(2,1)} %bitcast.31), custom_call_target="tpu_custom_call" | custom-call | flops 250000000 | bytes 1048576 | tf_op jit(solution)/shard_map/pallas_call | solution.py:316
  2.3 10.3 %all-to-all-start = ((bf16[16,8,1920]{2,1,0:T(8,128)(2,1)}), bf16[16,8,1920]{2,1,0:T(8,128)(2,1)S(1)}, u32[]{:S(2)}, u32[]{:S(2)}) async-start(bf16[16,8,1920]{2,1,0:T(8,128)(2,1)} %shard_map.94), calls=%async_computation | async-start | bytes 983040 | tf_op jit(solution)/shard_map/all_to_all | solution.py:346
  12.7 3.1 %collective-permute-start.1 = (bf16[16,1024]{1,0:T(8,128)(2,1)S(1)}, bf16[16,1024]{1,0:T(8,128)(2,1)S(1)}, u32[]{:S(2)}, u32[]{:S(2)}) collective-permute-start(bf16[16,1024]{1,0:T(8,128)(2,1)S(1)} %get-tuple-element.54), channel_id=1, source_target_pairs={{16,32},{48,64},{80,96},{112,128},{144,160},{176,192},{208,224},{2... | collective-permute-start | bytes 98312 | tf_op jit(solution)/shard_map/ppermute | solution.py:341
  15.7 1.9 %collective-permute-start = (bf16[16,1024]{1,0:T(8,128)(2,1)S(1)}, bf16[16,1024]{1,0:T(8,128)(2,1)S(1)}, u32[]{:S(2)}, u32[]{:S(2)}) collective-permute-start(bf16[16,1024]{1,0:T(8,128)(2,1)S(1)} %get-tuple-element.55), channel_id=1, source_target_pairs={{0,16},{16,0},{32,48},{48,32},{64,80},{80,64},{96,112},{112,96},{1... | collective-permute-start | bytes 98312 | tf_op jit(solution)/shard_map/ppermute | solution.py:340
  17.7 0.0 copy-start.1
  17.7 1.0 shard_map.92
  18.7 0.2 collective-permute-done.near
  18.8 0.8 shard_map.93
  19.6 9.6 %all-to-all-done = bf16[16,8,1920]{2,1,0:T(8,128)(2,1)S(1)} async-done(((bf16[16,8,1920]{2,1,0:T(8,128)(2,1)}), bf16[16,8,1920]{2,1,0:T(8,128)(2,1)S(1)}, u32[]{:S(2)}, u32[]{:S(2)}) %all-to-all-start) | async-done | bytes 491552 | tf_op jit(solution)/shard_map/all_to_all | solution.py:346
  29.2 4.2 %collective-permute-start.4 = (bf16[128,1920]{1,0:T(8,128)(2,1)S(1)}, bf16[128,1920]{1,0:T(8,128)(2,1)S(1)}, u32[]{:S(2)}, u32[]{:S(2)}) collective-permute-start(bf16[128,1920]{1,0:T(8,128)(2,1)S(1)} %bitcast.25), channel_id=1, source_target_pairs={{0,16},{16,0},{32,48},{48,32},{64,80},{80,64},{96,112},{112,96},{1... | collective-permute-start | bytes 1474568 | tf_op jit(solution)/shard_map/ppermute | solution.py:381
  33.5 0.0 copy-start
  33.5 2.2 %collective-permute-start.3 = (bf16[64,128]{1,0:T(8,128)(2,1)S(1)}, bf16[64,128]{1,0:T(8,128)(2,1)S(1)}, u32[]{:S(2)}, u32[]{:S(2)}) collective-permute-start(bf16[64,128]{1,0:T(8,128)(2,1)S(1)} %get-tuple-element.27.own.coarse_in), channel_id=1, source_target_pairs={{16,32},{48,64},{80,96},{112,128},{144,160},{176,192},{208,224},{2... | collective-permute-start | bytes 49160 | tf_op jit(solution)/shard_map/ppermute | solution.py:341
  35.7 1.9 %collective-permute-start.2 = (bf16[64,128]{1,0:T(8,128)(2,1)S(1)}, bf16[64,128]{1,0:T(8,128)(2,1)S(1)}, u32[]{:S(2)}, u32[]{:S(2)}) collective-permute-start(bf16[64,128]{1,0:T(8,128)(2,1)S(1)} %get-tuple-element.27.own.coarse_in), channel_id=1, source_target_pairs={{0,16},{16,0},{32,48},{48,32},{64,80},{80,64},{96,112},{112,96},{1... | collective-permute-start | bytes 49160 | tf_op jit(solution)/shard_map/ppermute | solution.py:340
  37.7 1.0 collective-permute-done.3.far
  38.7 0.1 collective-permute-done.2.near
  38.8 0.7 shard_map.95
  39.5 4.9 %collective-permute-start.6 = (bf16[64,128]{1,0:T(8,128)(2,1)S(1)}, bf16[64,128]{1,0:T(8,128)(2,1)S(1)}, u32[]{:S(2)}, u32[]{:S(2)}) collective-permute-start(bf16[64,128]{1,0:T(8,128)(2,1)S(1)} %get-tuple-element.30.own), channel_id=1, source_target_pairs={{16,32},{48,64},{80,96},{112,128},{144,160},{176,192},{208,224},{2... | collective-permute-start | bytes 49160 | tf_op jit(solution)/shard_map/ppermute | solution.py:341
  44.4 1.9 %collective-permute-start.5 = (bf16[64,128]{1,0:T(8,128)(2,1)S(1)}, bf16[64,128]{1,0:T(8,128)(2,1)S(1)}, u32[]{:S(2)}, u32[]{:S(2)}) collective-permute-start(bf16[64,128]{1,0:T(8,128)(2,1)S(1)} %get-tuple-element.30.own), channel_id=1, source_target_pairs={{0,16},{16,0},{32,48},{48,32},{64,80},{80,64},{96,112},{112,96},{1... | collective-permute-start | bytes 49160 | tf_op jit(solution)/shard_map/ppermute | solution.py:340
  46.4 1.1 collective-permute-done.5.near
  47.5 1.8 %shard_map.96 = (bf16[16,168,128]{2,1,0:T(8,128)(2,1)}, bf16[2,128,128]{2,1,0:T(8,128)(2,1)S(1)}) custom-call(s32[1]{0:T(128)} %bitcast.core, bf16[64,128]{1,0:T(8,128)(2,1)S(1)} %get-tuple-element.30.own, bf16[64,128]{1,0:T(8,128)(2,1)S(1)} %collective-permute-done.5.near, bf16[64,128]{1,0:T(8,128)(2,1)S(1)} %collective-permute-done.6.far, ...), custom_call_target="tpu_custom_call" | custom-call | flops 250000000 | bytes 1048576 | tf_op jit(solution)/shard_map/pallas_call | solution.py:316
  49.3 3.7 %all-to-all-start.1 = ((bf16[16,168,128]{2,1,0:T(8,128)(2,1)}), bf16[16,168,128]{2,1,0:T(8,128)(2,1)S(1)}, u32[]{:S(2)}, u32[]{:S(2)}) async-start(bf16[16,168,128]{2,1,0:T(8,128)(2,1)} %get-tuple-element.36), calls=%async_computation.1 | async-start | bytes 1376256 | tf_op jit(solution)/shard_map/all_to_all | solution.py:346
  53.1 2.1 %collective-permute-start.8 = (bf16[128,128]{1,0:T(8,128)(2,1)S(1)}, bf16[128,128]{1,0:T(8,128)(2,1)S(1)}, u32[]{:S(2)}, u32[]{:S(2)}) collective-permute-start(bf16[128,128]{1,0:T(8,128)(2,1)S(1)} %get-tuple-element.52), channel_id=1, source_target_pairs={{16,0},{32,16},{48,32},{64,48},{80,64},{96,80},{112,96},{128,112},... | collective-permute-start | bytes 98312 | tf_op jit(solution)/shard_map/ppermute | solution.py:334
  55.1 3.5 %collective-permute-start.7 = (bf16[128,128]{1,0:T(8,128)(2,1)S(1)}, bf16[128,128]{1,0:T(8,128)(2,1)S(1)}, u32[]{:S(2)}, u32[]{:S(2)}) collective-permute-start(bf16[128,128]{1,0:T(8,128)(2,1)S(1)} %get-tuple-element.53), channel_id=1, source_target_pairs={{0,16},{16,32},{32,48},{48,64},{64,80},{80,96},{96,112},{112,128},... | collective-permute-start | bytes 98312 | tf_op jit(solution)/shard_map/ppermute | solution.py:334
  58.6 1.0 collective-permute-done.7.before
  59.6 1.1 shard_map.97
  60.7 13.0 %all-to-all-done.1.parts = bf16[16,168,128]{2,1,0:T(8,128)(2,1)S(1)} async-done(((bf16[16,168,128]{2,1,0:T(8,128)(2,1)}), bf16[16,168,128]{2,1,0:T(8,128)(2,1)S(1)}, u32[]{:S(2)}, u32[]{:S(2)}) %all-to-all-start.1) | async-done | bytes 688160 | tf_op jit(solution)/shard_map/all_to_all | solution.py:346
  73.7 0.9 shard_map.98
  74.7 22.8 %all_to_all.25.terms = bf16[32,16,128]{2,1,0:T(8,128)(2,1)S(1)} all-to-all(bf16[32,16,128]{2,1,0:T(8,128)(2,1)S(1)} %get-tuple-element.42), channel_id=1, replica_groups=mesh['gz'=32,'grp'=16] {'gz'}, dimensions={0} | all-to-all | bytes 262144 | tf_op jit(solution)/shard_map/all_to_all | solution.py:346
  97.5 12.5 %all_to_all.26.terms = bf16[32,16,128]{2,1,0:T(8,128)(2,1)S(1)} all-to-all(bf16[32,16,128]{2,1,0:T(8,128)(2,1)S(1)} %shard_map.99), channel_id=1, replica_groups=mesh['gz'=32,'grp'=16] {'gz'}, dimensions={0} | all-to-all | bytes 262144 | tf_op jit(solution)/shard_map/all_to_all | solution.py:346
  110.1 0.7 shard_map.100
  110.8 17.1 %all_to_all.27 = bf16[16,88,128]{2,1,0:T(8,128)(2,1)S(1)} all-to-all(bf16[16,88,128]{2,1,0:T(8,128)(2,1)S(1)} %get-tuple-element.43), channel_id=1, replica_groups=mesh['gz'=32,'grp'=16] {'grp'}, dimensions={0} | all-to-all | bytes 720896 | tf_op jit(solution)/shard_map/all_to_all | solution.py:346
  127.9 0.9 shard_map.101
  (15 shorter events, 0.1 us)
Async XLA Ops:
  2.3 10.4 %copy-start.2 = (bf16[1,2,16,1024]{3,2,1,0:T(8,128)(2,1)S(1)}, bf16[1,2,16,1024]{3,2,1,0:T(8,128)(2,1)}, u32[]{:S(2)}) copy-start(bf16[1,2,16,1024]{3,2,1,0:T(8,128)(2,1)} %param.5) | copy-start | bytes 196612
  2.3 15.4 %copy-start.3 = (bf16[1728,64]{0,1:T(8,128)(2,1)S(1)}, bf16[1728,64]{0,1:T(8,128)(2,1)}, u32[]{:S(2)}) copy-start(bf16[1728,64]{0,1:T(8,128)(2,1)} %param.7) | copy-start | bytes 663556
  2.3 26.9 %all-to-all-start = ((bf16[16,8,1920]{2,1,0:T(8,128)(2,1)}), bf16[16,8,1920]{2,1,0:T(8,128)(2,1)S(1)}, u32[]{:S(2)}, u32[]{:S(2)}) async-start(bf16[16,8,1920]{2,1,0:T(8,128)(2,1)} %shard_map.94), calls=%async_computation | async-start | bytes 983040 | tf_op jit(solution)/shard_map/all_to_all | solution.py:346
  12.7 6.0 %collective-permute-start.1 = (bf16[16,1024]{1,0:T(8,128)(2,1)S(1)}, bf16[16,1024]{1,0:T(8,128)(2,1)S(1)}, u32[]{:S(2)}, u32[]{:S(2)}) collective-permute-start(bf16[16,1024]{1,0:T(8,128)(2,1)S(1)} %get-tuple-element.54), channel_id=1, source_target_pairs={{16,32},{48,64},{80,96},{112,128},{144,160},{176,192},{208,224},{2... | collective-permute-start | bytes 98312 | tf_op jit(solution)/shard_map/ppermute | solution.py:341
  15.7 3.1 %collective-permute-start = (bf16[16,1024]{1,0:T(8,128)(2,1)S(1)}, bf16[16,1024]{1,0:T(8,128)(2,1)S(1)}, u32[]{:S(2)}, u32[]{:S(2)}) collective-permute-start(bf16[16,1024]{1,0:T(8,128)(2,1)S(1)} %get-tuple-element.55), channel_id=1, source_target_pairs={{0,16},{16,0},{32,48},{48,32},{64,80},{80,64},{96,112},{112,96},{1... | collective-permute-start | bytes 98312 | tf_op jit(solution)/shard_map/ppermute | solution.py:340
  17.7 1.2 copy-start.1
  29.2 9.6 %collective-permute-start.4 = (bf16[128,1920]{1,0:T(8,128)(2,1)S(1)}, bf16[128,1920]{1,0:T(8,128)(2,1)S(1)}, u32[]{:S(2)}, u32[]{:S(2)}) collective-permute-start(bf16[128,1920]{1,0:T(8,128)(2,1)S(1)} %bitcast.25), channel_id=1, source_target_pairs={{0,16},{16,0},{32,48},{48,32},{64,80},{80,64},{96,112},{112,96},{1... | collective-permute-start | bytes 1474568 | tf_op jit(solution)/shard_map/ppermute | solution.py:381
  33.5 14.1 %copy-start = (bf16[4,128,256]{2,1,0:T(8,128)(2,1)S(1)}, bf16[4,128,256]{2,1,0:T(8,128)(2,1)}, u32[]{:S(2)}) copy-start(bf16[4,128,256]{2,1,0:T(8,128)(2,1)} %get-tuple-element.34.windows) | copy-start | bytes 786436
  33.5 5.2 %collective-permute-start.3 = (bf16[64,128]{1,0:T(8,128)(2,1)S(1)}, bf16[64,128]{1,0:T(8,128)(2,1)S(1)}, u32[]{:S(2)}, u32[]{:S(2)}) collective-permute-start(bf16[64,128]{1,0:T(8,128)(2,1)S(1)} %get-tuple-element.27.own.coarse_in), channel_id=1, source_target_pairs={{16,32},{48,64},{80,96},{112,128},{144,160},{176,192},{208,224},{2... | collective-permute-start | bytes 49160 | tf_op jit(solution)/shard_map/ppermute | solution.py:341
  35.7 3.1 %collective-permute-start.2 = (bf16[64,128]{1,0:T(8,128)(2,1)S(1)}, bf16[64,128]{1,0:T(8,128)(2,1)S(1)}, u32[]{:S(2)}, u32[]{:S(2)}) collective-permute-start(bf16[64,128]{1,0:T(8,128)(2,1)S(1)} %get-tuple-element.27.own.coarse_in), channel_id=1, source_target_pairs={{0,16},{16,0},{32,48},{48,32},{64,80},{80,64},{96,112},{112,96},{1... | collective-permute-start | bytes 49160 | tf_op jit(solution)/shard_map/ppermute | solution.py:340
  39.5 6.9 %collective-permute-start.6 = (bf16[64,128]{1,0:T(8,128)(2,1)S(1)}, bf16[64,128]{1,0:T(8,128)(2,1)S(1)}, u32[]{:S(2)}, u32[]{:S(2)}) collective-permute-start(bf16[64,128]{1,0:T(8,128)(2,1)S(1)} %get-tuple-element.30.own), channel_id=1, source_target_pairs={{16,32},{48,64},{80,96},{112,128},{144,160},{176,192},{208,224},{2... | collective-permute-start | bytes 49160 | tf_op jit(solution)/shard_map/ppermute | solution.py:341
  44.4 3.1 %collective-permute-start.5 = (bf16[64,128]{1,0:T(8,128)(2,1)S(1)}, bf16[64,128]{1,0:T(8,128)(2,1)S(1)}, u32[]{:S(2)}, u32[]{:S(2)}) collective-permute-start(bf16[64,128]{1,0:T(8,128)(2,1)S(1)} %get-tuple-element.30.own), channel_id=1, source_target_pairs={{0,16},{16,0},{32,48},{48,32},{64,80},{80,64},{96,112},{112,96},{1... | collective-permute-start | bytes 49160 | tf_op jit(solution)/shard_map/ppermute | solution.py:340
  49.3 10.3 %copy-start.4 = (bf16[9,256,128]{2,1,0:T(8,128)(2,1)S(1)}, bf16[9,256,128]{2,1,0:T(8,128)(2,1)}, u32[]{:S(2)}) copy-start(bf16[9,256,128]{2,1,0:T(8,128)(2,1)} %get-tuple-element.38.weights) | copy-start | bytes 1769476
  49.3 24.4 %all-to-all-start.1 = ((bf16[16,168,128]{2,1,0:T(8,128)(2,1)}), bf16[16,168,128]{2,1,0:T(8,128)(2,1)S(1)}, u32[]{:S(2)}, u32[]{:S(2)}) async-start(bf16[16,168,128]{2,1,0:T(8,128)(2,1)} %get-tuple-element.36), calls=%async_computation.1 | async-start | bytes 1376256 | tf_op jit(solution)/shard_map/all_to_all | solution.py:346
  53.1 5.6 %collective-permute-start.8 = (bf16[128,128]{1,0:T(8,128)(2,1)S(1)}, bf16[128,128]{1,0:T(8,128)(2,1)S(1)}, u32[]{:S(2)}, u32[]{:S(2)}) collective-permute-start(bf16[128,128]{1,0:T(8,128)(2,1)S(1)} %get-tuple-element.52), channel_id=1, source_target_pairs={{16,0},{32,16},{48,32},{64,48},{80,64},{96,80},{112,96},{128,112},... | collective-permute-start | bytes 98312 | tf_op jit(solution)/shard_map/ppermute | solution.py:334
  55.1 4.5 %collective-permute-start.7 = (bf16[128,128]{1,0:T(8,128)(2,1)S(1)}, bf16[128,128]{1,0:T(8,128)(2,1)S(1)}, u32[]{:S(2)}, u32[]{:S(2)}) collective-permute-start(bf16[128,128]{1,0:T(8,128)(2,1)S(1)} %get-tuple-element.53), channel_id=1, source_target_pairs={{0,16},{16,32},{32,48},{48,64},{64,80},{80,96},{96,112},{112,128},... | collective-permute-start | bytes 98312 | tf_op jit(solution)/shard_map/ppermute | solution.py:334

commit v2 on v1

--- a/solution.py
+++ b/solution.py
@@ -142,7 +142,17 @@
             out[at, :, 0:HALF] = kernel[:, 3456 - HALF : 3456]
 
 
-def coarse_forward(core, own, near, far, mine, other, grad, out, packed, scratch, sides):
+def insert_plane(mine, coarse_in, out):
+    out[:, 0:HALF] = mine[:, 0:HALF]
+    cotangent = mine[:, HALF : HALF + 128].astype(F32)[:, 0:64]
+    plane = coarse_in[...].astype(F32).T
+    out[:, HALF : HALF + 128] = jnp.concatenate([cotangent, plane], axis=1).astype(BF16)
+
+
+def coarse_forward(
+    core, own, far, mine, other, grad, out, packed, scratch, sides, near
+):
+    near[...] = other[:, HALF : HALF + 128].astype(F32).T[64:128].astype(BF16)
     sort_sides(core, near, far, sides)
     before, after = sides.at[0], sides.at[1]
     rest = 3456 - HALF
@@ -334,12 +344,17 @@
     return lax.ppermute(last, "gz", up), lax.ppermute(first, "gz", down)
 
 
+def core_swap(array):
+    return lax.ppermute(array, "gz", [(i, i ^ 1) for i in range(lax.axis_size("gz"))])
+
+
+def other_swap(array):
+    up = [(i, i + 1) for i in range(1, lax.axis_size("gz") - 1, 2)]
+    return lax.ppermute(array, "gz", up + [(j, i) for i, j in up])
+
+
 def pair_swaps(to_core, to_other):
-    devices = lax.axis_size("gz")
-    up = [(i, i + 1) for i in range(1, devices - 1, 2)]
-    near = lax.ppermute(to_core, "gz", [(i, i ^ 1) for i in range(devices)])
-    far = lax.ppermute(to_other, "gz", up + [(j, i) for i, j in up])
-    return near, far
+    return core_swap(to_core), other_swap(to_other)
 
 
 def exchange(blocks, axis):
@@ -374,16 +389,16 @@
         vol, near, far, ahead, down_kernel,
         scratch=[((256, 128), F32), ((2, 16, 1024), BF16)],
         core=core,
-        far=(2,),
-    )
-    in_near, in_far = pair_swaps(coarse_in, coarse_in)
-    mine, slope = lax.optimization_barrier((mine, slope))
-    other = lax.ppermute(mine, "gz", [(i, i ^ 1) for i in range(slabs)])
+        far=(1, 2),
+    )
+    in_far = other_swap(coarse_in)
+    (mine,) = call(insert_plane, [((128, HALF + 128), BF16)], mine, coarse_in)
+    other = core_swap(mine)
     coarse_grad, features, packed = call(
         coarse_forward,
         [((64, 128), BF16), ((128, 128), BF16), ((128, 3456), BF16)],
-        coarse_in, in_near, in_far, mine, other,
-        scratch=[((128, 128), F32), ((2, 64, 128), BF16)],
+        coarse_in, in_far, mine, other,
+        scratch=[((128, 128), F32), ((2, 64, 128), BF16), ((64, 128), BF16)],
         core=core,
     )
     grad_near, grad_far = pair_swaps(coarse_grad, coarse_grad)
@@ -396,6 +411,16 @@
         core=core,
     )
     parts = exchange(parts, "grp")
+    out_rows, terms = call(
+        coarse_kernel_terms,
+        [((group, 8, 64), BF16), ((slabs, 16, 128), BF16)],
+        parts,
+        scratch=[((72, 1024), F32), ((1024, 384), BF16)],
+        far=(0,),
+    )
+    terms = exchange(terms, "gz")
+    (terms,) = call(sum_slabs, [((slabs, 16, 128), BF16)], terms)
+    terms = exchange(terms, "gz")
     fine_before, fine_after = from_sides(fine_grad[1], fine_grad[0])
     (volume_grad,) = call(
         fine_backward,
@@ -404,17 +429,7 @@
         scratch=[((4, 128, 256), BF16)],
         far=(0,),
     )
-    parts, volume_grad = lax.optimization_barrier((parts, volume_grad))
-    out_rows, terms = call(
-        coarse_kernel_terms,
-        [((group, 8, 64), BF16), ((slabs, 16, 128), BF16)],
-        parts,
-        scratch=[((72, 1024), F32), ((1024, 384), BF16)],
-        far=(0,),
-    )
-    terms = exchange(terms, "gz")
-    (terms,) = call(sum_slabs, [((slabs, 16, 128), BF16)], terms)
-    terms = exchange(terms, "gz")
+    terms, volume_grad = lax.optimization_barrier((terms, volume_grad))
     coarse_kg, shared = call(collect, [((8, 3456), F32), ((group, 88, 128), BF16)], terms, far=(0,))
     shared = exchange(shared, "grp").reshape(1408, 128)
     fine_kg, down_kg = call(unpack, [((64, 1728), F32), ((512, 128), F32)], shared, far=(0, 1))

time: 130 us -> 129 us (level)
  blocking collectives: 52.5 us -> 66 us
  waiting for transfers between devices: 26 us -> 16.1 us
  starting transfers between devices: 39.9 us -> 35.4 us
    all_to_all x3, blocking collectives: 52.5 us -> 66 us  [exchange(): return lax.all_to_all(blocks, axis, 0, 0, tiled=True)]
    all_to_all x2, waiting for transfers between devices: 22.6 us -> 10.9 us  [exchange(): return lax.all_to_all(blocks, axis, 0, 0, tiled=True)]
    ppermute x7 -> x6, starting transfers between devices: 20.2 us -> 15.5 us  [the longest x3 8.21 us: core_swap(): lax.ppermute(array, 'gz', [(i, i ^ 1) for i in range(lax.axis_size('gz'))])]
    ppermute x7 -> x6, waiting for transfers between devices: 2.46 us -> 4.22 us  [the longest x3 3.93 us: other_swap(): return lax.ppermute(array, 'gz', up + [(j, i) for i, j in up])]
    pallas_call x10 -> x11, Pallas kernels: 9.57 us -> 10.1 us  [call(): pl.pallas_call(body, out_shape=[put(*out) for put, out in zip(place, outs...]
  transfers between devices with their start and end apart: 11 -> 10, of which waited for: 7 -> 8; matrix products, arithmetic and copies ran while one was open for 0% -> 0% of each run, Pallas kernels for 2% -> 3%
where the time goes in v2:
time: 129 us; the launch traced here: 128 us
  blocking collectives  66 us (51%)
  starting transfers between devices  35.4 us (27%)
  waiting for transfers between devices  16.1 us (12%)
  Pallas kernels  10.1 us (8%)
    all_to_all x3, blocking collectives, exchange(): return lax.all_to_all(blocks, axis, 0, 0, tiled=True)  66 us
    all_to_all x2, starting transfers between devices, exchange(): return lax.all_to_all(blocks, axis, 0, 0, tiled=True)  14.3 us
    all_to_all x2, waiting for transfers between devices, exchange(): return lax.all_to_all(blocks, axis, 0, 0, tiled=True)  10.9 us
    pallas_call x11, Pallas kernels, call(): pl.pallas_call(body, out_shape=[put(*out) for put, out in zip(place, outs...  10.1 us
    ppermute x3, starting transfers between devices, core_swap(): lax.ppermute(array, 'gz', [(i, i ^ 1) for i in range(lax.axis_size('gz'))])  8.21 us
    ppermute x3, starting transfers between devices, other_swap(): return lax.ppermute(array, 'gz', up + [(j, i) for i, j in up])  7.31 us
    ppermute x2, starting transfers between devices, from_sides(): return (lax.ppermute(last, 'gz', up), lax.ppermute(first, 'gz', down))  5.56 us
    ppermute x3, waiting for transfers between devices, other_swap(): return lax.ppermute(array, 'gz', up + [(j, i) for i, j in up])  3.93 us
  transfers between devices with their start and end apart: 10, of which 8 were waited for; matrix products, arithmetic and copies ran while one was open for 0% of the time, Pallas kernels for 3%

profile of v2, /device:TPU:1, one launch (start us, length us, event | category | flops | bytes accessed | tf_op | source)
XLA Modules:
  0.0 128.4 jit_solution(15388305303383348257)
XLA Ops:
  0.6 1.7 %shard_map.94 = bf16[16,8,1920]{2,1,0:T(8,128)(2,1)} custom-call(s32[1]{0:T(128)} %bitcast.core, bf16[8,3456]{1,0:T(8,128)(2,1)} %bitcast.29, bf16[16,8,64]{2,1,0:T(8,128)(2,1)} %bitcast.30), custom_call_target="tpu_custom_call" | custom-call | flops 250000000 | bytes 1048576 | tf_op jit(solution)/shard_map/pallas_call | solution.py:326
  2.3 10.3 %all-to-all-start = ((bf16[16,8,1920]{2,1,0:T(8,128)(2,1)}), bf16[16,8,1920]{2,1,0:T(8,128)(2,1)S(1)}, u32[]{:S(2)}, u32[]{:S(2)}) async-start(bf16[16,8,1920]{2,1,0:T(8,128)(2,1)} %shard_map.94), calls=%async_computation | async-start | bytes 983040 | tf_op jit(solution)/shard_map/all_to_all | solution.py:361
  12.7 3.1 %collective-permute-start.1 = (bf16[16,1024]{1,0:T(8,128)(2,1)S(1)}, bf16[16,1024]{1,0:T(8,128)(2,1)S(1)}, u32[]{:S(2)}, u32[]{:S(2)}) collective-permute-start(bf16[16,1024]{1,0:T(8,128)(2,1)S(1)} %get-tuple-element.50), channel_id=1, source_target_pairs={{16,32},{48,64},{80,96},{112,128},{144,160},{176,192},{208,224},{2... | collective-permute-start | bytes 98312 | tf_op jit(solution)/shard_map/ppermute | solution.py:353
  15.7 1.9 %collective-permute-start = (bf16[16,1024]{1,0:T(8,128)(2,1)S(1)}, bf16[16,1024]{1,0:T(8,128)(2,1)S(1)}, u32[]{:S(2)}, u32[]{:S(2)}) collective-permute-start(bf16[16,1024]{1,0:T(8,128)(2,1)S(1)} %get-tuple-element.51), channel_id=1, source_target_pairs={{0,16},{16,0},{32,48},{48,32},{64,80},{80,64},{96,112},{112,96},{1... | collective-permute-start | bytes 98312 | tf_op jit(solution)/shard_map/ppermute | solution.py:348
  17.7 1.0 shard_map.92
  18.7 0.1 collective-permute-done.near
  18.9 1.2 shard_map.93
  20.0 9.2 %all-to-all-done = bf16[16,8,1920]{2,1,0:T(8,128)(2,1)S(1)} async-done(((bf16[16,8,1920]{2,1,0:T(8,128)(2,1)}), bf16[16,8,1920]{2,1,0:T(8,128)(2,1)S(1)}, u32[]{:S(2)}, u32[]{:S(2)}) %all-to-all-start) | async-done | bytes 491552 | tf_op jit(solution)/shard_map/all_to_all | solution.py:361
  29.2 0.2 shard_map.95.mine
  29.4 4.4 %collective-permute-start.3 = (bf16[128,1920]{1,0:T(8,128)(2,1)S(1)}, bf16[128,1920]{1,0:T(8,128)(2,1)S(1)}, u32[]{:S(2)}, u32[]{:S(2)}) collective-permute-start(bf16[128,1920]{1,0:T(8,128)(2,1)S(1)} %shard_map.95.mine), channel_id=1, source_target_pairs={{0,16},{16,0},{32,48},{48,32},{64,80},{80,64},{96,112},{112,96},{1... | collective-permute-start | bytes 1474568 | tf_op jit(solution)/shard_map/ppermute | solution.py:348
  33.8 2.1 %collective-permute-start.2 = (bf16[64,128]{1,0:T(8,128)(2,1)S(1)}, bf16[64,128]{1,0:T(8,128)(2,1)S(1)}, u32[]{:S(2)}, u32[]{:S(2)}) collective-permute-start(bf16[64,128]{1,0:T(8,128)(2,1)S(1)} %get-tuple-element.25.coarse_in.own), channel_id=1, source_target_pairs={{16,32},{48,64},{80,96},{112,128},{144,160},{176,192},{208,224},{2... | collective-permute-start | bytes 49160 | tf_op jit(solution)/shard_map/ppermute | solution.py:353
  35.9 2.9 %collective-permute-done.2.far = bf16[64,128]{1,0:T(8,128)(2,1)S(1)} collective-permute-done((bf16[64,128]{1,0:T(8,128)(2,1)S(1)}, bf16[64,128]{1,0:T(8,128)(2,1)S(1)}, u32[]{:S(2)}, u32[]{:S(2)}) %collective-permute-start.2) | collective-permute-done | bytes 16416 | tf_op jit(solution)/shard_map/ppermute | solution.py:353
  38.9 0.8 shard_map.96
  39.7 2.1 %collective-permute-start.5 = (bf16[64,128]{1,0:T(8,128)(2,1)S(1)}, bf16[64,128]{1,0:T(8,128)(2,1)S(1)}, u32[]{:S(2)}, u32[]{:S(2)}) collective-permute-start(bf16[64,128]{1,0:T(8,128)(2,1)S(1)} %get-tuple-element.26.own), channel_id=1, source_target_pairs={{16,32},{48,64},{80,96},{112,128},{144,160},{176,192},{208,224},{2... | collective-permute-start | bytes 49160 | tf_op jit(solution)/shard_map/ppermute | solution.py:353
  41.8 1.9 %collective-permute-start.4 = (bf16[64,128]{1,0:T(8,128)(2,1)S(1)}, bf16[64,128]{1,0:T(8,128)(2,1)S(1)}, u32[]{:S(2)}, u32[]{:S(2)}) collective-permute-start(bf16[64,128]{1,0:T(8,128)(2,1)S(1)} %get-tuple-element.26.own), channel_id=1, source_target_pairs={{0,16},{16,0},{32,48},{48,32},{64,80},{80,64},{96,112},{112,96},{1... | collective-permute-start | bytes 49160 | tf_op jit(solution)/shard_map/ppermute | solution.py:348
  43.7 1.0 collective-permute-done.5.far
  44.7 0.2 collective-permute-done.4.near
  44.9 0.9 shard_map.97
  45.8 25.3 %all_to_all.25.parts = bf16[16,168,128]{2,1,0:T(8,128)(2,1)S(1)} all-to-all(bf16[16,168,128]{2,1,0:T(8,128)(2,1)S(1)} %get-tuple-element.32), channel_id=1, replica_groups=mesh['gz'=32,'grp'=16] {'grp'}, dimensions={0} | all-to-all | bytes 1376256 | tf_op jit(solution)/shard_map/all_to_all | solution.py:361
  71.1 0.9 shard_map.98
  72.0 23.7 %all_to_all.26.terms = bf16[32,16,128]{2,1,0:T(8,128)(2,1)S(1)} all-to-all(bf16[32,16,128]{2,1,0:T(8,128)(2,1)S(1)} %get-tuple-element.34), channel_id=1, replica_groups=mesh['gz'=32,'grp'=16] {'gz'}, dimensions={0} | all-to-all | bytes 262144 | tf_op jit(solution)/shard_map/all_to_all | solution.py:361
  95.7 0.7 shard_map.99
  96.4 4.0 %all-to-all-start.3 = ((bf16[32,16,128]{2,1,0:T(8,128)(2,1)}), bf16[32,16,128]{2,1,0:T(8,128)(2,1)S(1)}, u32[]{:S(2)}, u32[]{:S(2)}) async-start(bf16[32,16,128]{2,1,0:T(8,128)(2,1)} %shard_map.99), calls=%async_computation.3 | async-start | bytes 262144 | tf_op jit(solution)/shard_map/all_to_all | solution.py:361
  100.4 2.3 %collective-permute-start.7 = (bf16[128,128]{1,0:T(8,128)(2,1)S(1)}, bf16[128,128]{1,0:T(8,128)(2,1)S(1)}, u32[]{:S(2)}, u32[]{:S(2)}) collective-permute-start(bf16[128,128]{1,0:T(8,128)(2,1)S(1)} %get-tuple-element.48), channel_id=1, source_target_pairs={{16,0},{32,16},{48,32},{64,48},{80,64},{96,80},{112,96},{128,112},... | collective-permute-start | bytes 98312 | tf_op jit(solution)/shard_map/ppermute | solution.py:344
  102.7 3.3 %collective-permute-start.6 = (bf16[128,128]{1,0:T(8,128)(2,1)S(1)}, bf16[128,128]{1,0:T(8,128)(2,1)S(1)}, u32[]{:S(2)}, u32[]{:S(2)}) collective-permute-start(bf16[128,128]{1,0:T(8,128)(2,1)S(1)} %get-tuple-element.49), channel_id=1, source_target_pairs={{0,16},{16,32},{32,48},{48,64},{64,80},{80,96},{96,112},{112,128},... | collective-permute-start | bytes 98312 | tf_op jit(solution)/shard_map/ppermute | solution.py:344
  106.0 0.1 collective-permute-done.7.after
  106.1 0.9 collective-permute-done.6.before
  107.0 1.1 shard_map.100
  108.1 1.7 %all-to-all-done.3.terms = bf16[32,16,128]{2,1,0:T(8,128)(2,1)S(1)} async-done(((bf16[32,16,128]{2,1,0:T(8,128)(2,1)}), bf16[32,16,128]{2,1,0:T(8,128)(2,1)S(1)}, u32[]{:S(2)}, u32[]{:S(2)}) %all-to-all-start.3) | async-done | bytes 131104 | tf_op jit(solution)/shard_map/all_to_all | solution.py:361
  109.8 0.7 shard_map.101
  110.5 17.0 %all_to_all.27 = bf16[16,88,128]{2,1,0:T(8,128)(2,1)S(1)} all-to-all(bf16[16,88,128]{2,1,0:T(8,128)(2,1)S(1)} %get-tuple-element.39), channel_id=1, replica_groups=mesh['gz'=32,'grp'=16] {'grp'}, dimensions={0} | all-to-all | bytes 720896 | tf_op jit(solution)/shard_map/all_to_all | solution.py:361
  127.6 0.9 shard_map.102
  (16 shorter events, 0.1 us)
Async XLA Ops:
  2.3 10.4 %copy-start.3 = (bf16[1,2,16,1024]{3,2,1,0:T(8,128)(2,1)S(1)}, bf16[1,2,16,1024]{3,2,1,0:T(8,128)(2,1)}, u32[]{:S(2)}) copy-start(bf16[1,2,16,1024]{3,2,1,0:T(8,128)(2,1)} %param.5) | copy-start | bytes 196612
  2.3 15.4 %copy-start.4 = (bf16[1728,64]{0,1:T(8,128)(2,1)S(1)}, bf16[1728,64]{0,1:T(8,128)(2,1)}, u32[]{:S(2)}) copy-start(bf16[1728,64]{0,1:T(8,128)(2,1)} %param.7) | copy-start | bytes 663556
  2.3 26.9 %all-to-all-start = ((bf16[16,8,1920]{2,1,0:T(8,128)(2,1)}), bf16[16,8,1920]{2,1,0:T(8,128)(2,1)S(1)}, u32[]{:S(2)}, u32[]{:S(2)}) async-start(bf16[16,8,1920]{2,1,0:T(8,128)(2,1)} %shard_map.94), calls=%async_computation | async-start | bytes 983040 | tf_op jit(solution)/shard_map/all_to_all | solution.py:361
  12.7 6.0 %collective-permute-start.1 = (bf16[16,1024]{1,0:T(8,128)(2,1)S(1)}, bf16[16,1024]{1,0:T(8,128)(2,1)S(1)}, u32[]{:S(2)}, u32[]{:S(2)}) collective-permute-start(bf16[16,1024]{1,0:T(8,128)(2,1)S(1)} %get-tuple-element.50), channel_id=1, source_target_pairs={{16,32},{48,64},{80,96},{112,128},{144,160},{176,192},{208,224},{2... | collective-permute-start | bytes 98312 | tf_op jit(solution)/shard_map/ppermute | solution.py:353
  15.7 3.1 %collective-permute-start = (bf16[16,1024]{1,0:T(8,128)(2,1)S(1)}, bf16[16,1024]{1,0:T(8,128)(2,1)S(1)}, u32[]{:S(2)}, u32[]{:S(2)}) collective-permute-start(bf16[16,1024]{1,0:T(8,128)(2,1)S(1)} %get-tuple-element.51), channel_id=1, source_target_pairs={{0,16},{16,0},{32,48},{48,32},{64,80},{80,64},{96,112},{112,96},{1... | collective-permute-start | bytes 98312 | tf_op jit(solution)/shard_map/ppermute | solution.py:348
  17.7 1.2 copy-start.1
  29.4 15.5 %copy-start = (bf16[4,128,256]{2,1,0:T(8,128)(2,1)S(1)}, bf16[4,128,256]{2,1,0:T(8,128)(2,1)}, u32[]{:S(2)}) copy-start(bf16[4,128,256]{2,1,0:T(8,128)(2,1)} %get-tuple-element.30.windows) | copy-start | bytes 786436
  29.4 15.5 %copy-start.2 = (f32[256,128]{1,0:T(8,128)S(1)}, f32[256,128]{1,0:T(8,128)}, u32[]{:S(2)}) copy-start(f32[256,128]{1,0:T(8,128)} %get-tuple-element.29.slope) | copy-start | bytes 393220
  29.4 9.4 %collective-permute-start.3 = (bf16[128,1920]{1,0:T(8,128)(2,1)S(1)}, bf16[128,1920]{1,0:T(8,128)(2,1)S(1)}, u32[]{:S(2)}, u32[]{:S(2)}) collective-permute-start(bf16[128,1920]{1,0:T(8,128)(2,1)S(1)} %shard_map.95.mine), channel_id=1, source_target_pairs={{0,16},{16,0},{32,48},{48,32},{64,80},{80,64},{96,112},{112,96},{1... | collective-permute-start | bytes 1474568 | tf_op jit(solution)/shard_map/ppermute | solution.py:348
  33.8 5.1 %collective-permute-start.2 = (bf16[64,128]{1,0:T(8,128)(2,1)S(1)}, bf16[64,128]{1,0:T(8,128)(2,1)S(1)}, u32[]{:S(2)}, u32[]{:S(2)}) collective-permute-start(bf16[64,128]{1,0:T(8,128)(2,1)S(1)} %get-tuple-element.25.coarse_in.own), channel_id=1, source_target_pairs={{16,32},{48,64},{80,96},{112,128},{144,160},{176,192},{208,224},{2... | collective-permute-start | bytes 49160 | tf_op jit(solution)/shard_map/ppermute | solution.py:353
  39.7 5.1 %collective-permute-start.5 = (bf16[64,128]{1,0:T(8,128)(2,1)S(1)}, bf16[64,128]{1,0:T(8,128)(2,1)S(1)}, u32[]{:S(2)}, u32[]{:S(2)}) collective-permute-start(bf16[64,128]{1,0:T(8,128)(2,1)S(1)} %get-tuple-element.26.own), channel_id=1, source_target_pairs={{16,32},{48,64},{80,96},{112,128},{144,160},{176,192},{208,224},{2... | collective-permute-start | bytes 49160 | tf_op jit(solution)/shard_map/ppermute | solution.py:353
  41.8 3.1 %collective-permute-start.4 = (bf16[64,128]{1,0:T(8,128)(2,1)S(1)}, bf16[64,128]{1,0:T(8,128)(2,1)S(1)}, u32[]{:S(2)}, u32[]{:S(2)}) collective-permute-start(bf16[64,128]{1,0:T(8,128)(2,1)S(1)} %get-tuple-element.26.own), channel_id=1, source_target_pairs={{0,16},{16,0},{32,48},{48,32},{64,80},{80,64},{96,112},{112,96},{1... | collective-permute-start | bytes 49160 | tf_op jit(solution)/shard_map/ppermute | solution.py:348
  95.7 11.3 %copy-start.5 = (bf16[9,256,128]{2,1,0:T(8,128)(2,1)S(1)}, bf16[9,256,128]{2,1,0:T(8,128)(2,1)}, u32[]{:S(2)}) copy-start(bf16[9,256,128]{2,1,0:T(8,128)(2,1)} %get-tuple-element.36.weights) | copy-start | bytes 1769476
  96.4 13.4 %all-to-all-start.3 = ((bf16[32,16,128]{2,1,0:T(8,128)(2,1)}), bf16[32,16,128]{2,1,0:T(8,128)(2,1)S(1)}, u32[]{:S(2)}, u32[]{:S(2)}) async-start(bf16[32,16,128]{2,1,0:T(8,128)(2,1)} %shard_map.99), calls=%async_computation.3 | async-start | bytes 262144 | tf_op jit(solution)/shard_map/all_to_all | solution.py:361
  100.4 5.7 %collective-permute-start.7 = (bf16[128,128]{1,0:T(8,128)(2,1)S(1)}, bf16[128,128]{1,0:T(8,128)(2,1)S(1)}, u32[]{:S(2)}, u32[]{:S(2)}) collective-permute-start(bf16[128,128]{1,0:T(8,128)(2,1)S(1)} %get-tuple-element.48), channel_id=1, source_target_pairs={{16,0},{32,16},{48,32},{64,48},{80,64},{96,80},{112,96},{128,112},... | collective-permute-start | bytes 98312 | tf_op jit(solution)/shard_map/ppermute | solution.py:344
  102.7 4.3 %collective-permute-start.6 = (bf16[128,128]{1,0:T(8,128)(2,1)S(1)}, bf16[128,128]{1,0:T(8,128)(2,1)S(1)}, u32[]{:S(2)}, u32[]{:S(2)}) collective-permute-start(bf16[128,128]{1,0:T(8,128)(2,1)S(1)} %get-tuple-element.49), channel_id=1, source_target_pairs={{0,16},{16,32},{32,48},{48,64},{64,80},{80,96},{96,112},{112,128},... | collective-permute-start | bytes 98312 | tf_op jit(solution)/shard_map/ppermute | solution.py:344

commit v3 on v2

--- a/solution.py
+++ b/solution.py
@@ -277,14 +277,16 @@
         out[at, 80:168] = shared[at * 88 : at * 88 + 88].astype(BF16)
 
 
-def fine_backward(grad, before, after, weights, out, windows):
+def fine_backward(core, grad, near, far, weights, out, windows, sides):
+    sort_sides(core, near, far, sides)
+
     def blocks(plane):
         return [plane[j * 16 : (j + 1) * 16] for j in range(8)]
 
-    fill_windows(windows, 0, blocks(before[...]))
+    fill_windows(windows, 0, blocks(sides[0]))
     fill_windows(windows, 1, blocks(grad[0]))
     fill_windows(windows, 2, blocks(grad[1]))
-    fill_windows(windows, 3, blocks(after[...]))
+    fill_windows(windows, 3, blocks(sides[1]))
     total = window_conv(windows, weights, NN).astype(BF16)
     for z in range(2):
         for j in range(8):
@@ -337,13 +339,6 @@
 WORK = 250_000_000
 
 
-def from_sides(last, first):
-    devices = lax.axis_size("gz")
-    up = [(i, i + 1) for i in range(devices - 1)]
-    down = [(j, i) for i, j in up]
-    return lax.ppermute(last, "gz", up), lax.ppermute(first, "gz", down)
-
-
 def core_swap(array):
     return lax.ppermute(array, "gz", [(i, i ^ 1) for i in range(lax.axis_size("gz"))])
 
@@ -411,6 +406,19 @@
         core=core,
     )
     parts = exchange(parts, "grp")
+    fine_near, fine_far = pair_swaps(
+        lax.dynamic_index_in_dim(fine_grad, 1 - index, 0, keepdims=False),
+        lax.dynamic_index_in_dim(fine_grad, index, 0, keepdims=False),
+    )
+    (volume_grad,) = call(
+        fine_backward,
+        [((2, 16, 1024), BF16)],
+        fine_grad, fine_near, fine_far, behind,
+        scratch=[((4, 128, 256), BF16), ((2, 128, 128), BF16)],
+        core=core,
+        far=(0,),
+    )
+    parts, volume_grad = lax.optimization_barrier((parts, volume_grad))
     out_rows, terms = call(
         coarse_kernel_terms,
         [((group, 8, 64), BF16), ((slabs, 16, 128), BF16)],
@@ -421,15 +429,6 @@
     terms = exchange(terms, "gz")
     (terms,) = call(sum_slabs, [((slabs, 16, 128), BF16)], terms)
     terms = exchange(terms, "gz")
-    fine_before, fine_after = from_sides(fine_grad[1], fine_grad[0])
-    (volume_grad,) = call(
-        fine_backward,
-        [((2, 16, 1024), BF16)],
-        fine_grad, fine_before, fine_after, behind,
-        scratch=[((4, 128, 256), BF16)],
-        far=(0,),
-    )
-    terms, volume_grad = lax.optimization_barrier((terms, volume_grad))
     coarse_kg, shared = call(collect, [((8, 3456), F32), ((group, 88, 128), BF16)], terms, far=(0,))
     shared = exchange(shared, "grp").reshape(1408, 128)
     fine_kg, down_kg = call(unpack, [((64, 1728), F32), ((512, 128), F32)], shared, far=(0, 1))

time: 129 us -> 130 us (level)
  blocking collectives: 66 us -> 55.3 us
  waiting for transfers between devices: 16.1 us -> 25.1 us
  starting transfers between devices: 35.4 us -> 37.3 us
    all_to_all x3, blocking collectives: 66 us -> 55.3 us  [exchange(): return lax.all_to_all(blocks, axis, 0, 0, tiled=True)]
    all_to_all x2, waiting for transfers between devices: 10.9 us -> 19.7 us  [exchange(): return lax.all_to_all(blocks, axis, 0, 0, tiled=True)]
    ppermute x3 -> x4, starting transfers between devices: 7.31 us -> 13.1 us  [other_swap(): return lax.ppermute(array, 'gz', up + [(j, i) for i, j in up])]
    ppermute x2 -> x0, starting transfers between devices: 5.56 us -> none  [from_sides(): return (lax.ppermute(last, 'gz', up), lax.ppermute(first, 'gz', down))]
    ppermute x3 -> x4, starting transfers between devices: 8.21 us -> 10.1 us  [core_swap(): lax.ppermute(array, 'gz', [(i, i ^ 1) for i in range(lax.axis_size('gz'))])]
    ppermute x3 -> x4, waiting for transfers between devices: 3.93 us -> 3.95 us  [other_swap(): return lax.ppermute(array, 'gz', up + [(j, i) for i, j in up])]
  transfers between devices with their start and end apart: 10 -> 10, of which waited for: 8 -> 7; matrix products, arithmetic and copies ran while one was open for 0% -> 0% of each run, Pallas kernels for 3% -> 3%
where the time goes in v3:
time: 130 us; the launch traced here: 129 us
  blocking collectives  55.3 us (43%)
  starting transfers between devices  37.3 us (29%)
  waiting for transfers between devices  25.1 us (19%)
  Pallas kernels  10.3 us (8%)
    all_to_all x3, blocking collectives, exchange(): return lax.all_to_all(blocks, axis, 0, 0, tiled=True)  55.3 us
    all_to_all x2, waiting for transfers between devices, exchange(): return lax.all_to_all(blocks, axis, 0, 0, tiled=True)  19.7 us
    all_to_all x2, starting transfers between devices, exchange(): return lax.all_to_all(blocks, axis, 0, 0, tiled=True)  14.1 us
    ppermute x4, starting transfers between devices, other_swap(): return lax.ppermute(array, 'gz', up + [(j, i) for i, j in up])  13.1 us
    pallas_call x11, Pallas kernels, call(): pl.pallas_call(body, out_shape=[put(*out) for put, out in zip(place, outs...  10.3 us
    ppermute x4, starting transfers between devices, core_swap(): lax.ppermute(array, 'gz', [(i, i ^ 1) for i in range(lax.axis_size('gz'))])  10.1 us
    ppermute x4, waiting for transfers between devices, other_swap(): return lax.ppermute(array, 'gz', up + [(j, i) for i, j in up])  3.95 us
  transfers between devices with their start and end apart: 10, of which 7 were waited for; matrix products, arithmetic and copies ran while one was open for 0% of the time, Pallas kernels for 3%

profile of v3, /device:TPU:1, one launch (start us, length us, event | category | flops | bytes accessed | tf_op | source)
XLA Modules:
  0.0 128.8 jit_solution(9447425208875351924)
XLA Ops:
  0.6 1.7 %shard_map.94 = bf16[16,8,1920]{2,1,0:T(8,128)(2,1)} custom-call(s32[1]{0:T(128)} %bitcast.core, bf16[8,3456]{1,0:T(8,128)(2,1)} %bitcast.29, bf16[16,8,64]{2,1,0:T(8,128)(2,1)} %bitcast.30), custom_call_target="tpu_custom_call" | custom-call | flops 250000000 | bytes 1048576 | tf_op jit(solution)/shard_map/pallas_call | solution.py:328
  2.3 10.3 %all-to-all-start = ((bf16[16,8,1920]{2,1,0:T(8,128)(2,1)}), bf16[16,8,1920]{2,1,0:T(8,128)(2,1)S(1)}, u32[]{:S(2)}, u32[]{:S(2)}) async-start(bf16[16,8,1920]{2,1,0:T(8,128)(2,1)} %shard_map.94), calls=%async_computation | async-start | bytes 983040 | tf_op jit(solution)/shard_map/all_to_all | solution.py:356
  12.7 3.1 %collective-permute-start.1 = (bf16[16,1024]{1,0:T(8,128)(2,1)S(1)}, bf16[16,1024]{1,0:T(8,128)(2,1)S(1)}, u32[]{:S(2)}, u32[]{:S(2)}) collective-permute-start(bf16[16,1024]{1,0:T(8,128)(2,1)S(1)} %get-tuple-element.50), channel_id=1, source_target_pairs={{16,32},{48,64},{80,96},{112,128},{144,160},{176,192},{208,224},{2... | collective-permute-start | bytes 98312 | tf_op jit(solution)/shard_map/ppermute | solution.py:348
  15.7 1.9 %collective-permute-start = (bf16[16,1024]{1,0:T(8,128)(2,1)S(1)}, bf16[16,1024]{1,0:T(8,128)(2,1)S(1)}, u32[]{:S(2)}, u32[]{:S(2)}) collective-permute-start(bf16[16,1024]{1,0:T(8,128)(2,1)S(1)} %get-tuple-element.51), channel_id=1, source_target_pairs={{0,16},{16,0},{32,48},{48,32},{64,80},{80,64},{96,112},{112,96},{1... | collective-permute-start | bytes 98312 | tf_op jit(solution)/shard_map/ppermute | solution.py:343
  17.7 0.0 copy-start.1
  17.7 1.0 shard_map.92
  18.7 0.2 collective-permute-done.near
  18.8 1.2 shard_map.93
  20.0 9.2 %all-to-all-done = bf16[16,8,1920]{2,1,0:T(8,128)(2,1)S(1)} async-done(((bf16[16,8,1920]{2,1,0:T(8,128)(2,1)}), bf16[16,8,1920]{2,1,0:T(8,128)(2,1)S(1)}, u32[]{:S(2)}, u32[]{:S(2)}) %all-to-all-start) | async-done | bytes 491552 | tf_op jit(solution)/shard_map/all_to_all | solution.py:356
  29.2 0.2 shard_map.95.mine
  29.4 0.0 copy-start.2
  29.4 4.4 %collective-permute-start.3 = (bf16[128,1920]{1,0:T(8,128)(2,1)S(1)}, bf16[128,1920]{1,0:T(8,128)(2,1)S(1)}, u32[]{:S(2)}, u32[]{:S(2)}) collective-permute-start(bf16[128,1920]{1,0:T(8,128)(2,1)S(1)} %shard_map.95.mine), channel_id=1, source_target_pairs={{0,16},{16,0},{32,48},{48,32},{64,80},{80,64},{96,112},{112,96},{1... | collective-permute-start | bytes 1474568 | tf_op jit(solution)/shard_map/ppermute | solution.py:343
  33.8 2.1 %collective-permute-start.2 = (bf16[64,128]{1,0:T(8,128)(2,1)S(1)}, bf16[64,128]{1,0:T(8,128)(2,1)S(1)}, u32[]{:S(2)}, u32[]{:S(2)}) collective-permute-start(bf16[64,128]{1,0:T(8,128)(2,1)S(1)} %get-tuple-element.25.coarse_in.own), channel_id=1, source_target_pairs={{16,32},{48,64},{80,96},{112,128},{144,160},{176,192},{208,224},{2... | collective-permute-start | bytes 49160 | tf_op jit(solution)/shard_map/ppermute | solution.py:348
  35.9 2.9 %collective-permute-done.2.far = bf16[64,128]{1,0:T(8,128)(2,1)S(1)} collective-permute-done((bf16[64,128]{1,0:T(8,128)(2,1)S(1)}, bf16[64,128]{1,0:T(8,128)(2,1)S(1)}, u32[]{:S(2)}, u32[]{:S(2)}) %collective-permute-start.2) | collective-permute-done | bytes 16416 | tf_op jit(solution)/shard_map/ppermute | solution.py:348
  38.9 0.8 shard_map.96
  39.7 2.1 %collective-permute-start.5 = (bf16[64,128]{1,0:T(8,128)(2,1)S(1)}, bf16[64,128]{1,0:T(8,128)(2,1)S(1)}, u32[]{:S(2)}, u32[]{:S(2)}) collective-permute-start(bf16[64,128]{1,0:T(8,128)(2,1)S(1)} %get-tuple-element.26.own), channel_id=1, source_target_pairs={{16,32},{48,64},{80,96},{112,128},{144,160},{176,192},{208,224},{2... | collective-permute-start | bytes 49160 | tf_op jit(solution)/shard_map/ppermute | solution.py:348
  41.8 1.9 %collective-permute-start.4 = (bf16[64,128]{1,0:T(8,128)(2,1)S(1)}, bf16[64,128]{1,0:T(8,128)(2,1)S(1)}, u32[]{:S(2)}, u32[]{:S(2)}) collective-permute-start(bf16[64,128]{1,0:T(8,128)(2,1)S(1)} %get-tuple-element.26.own), channel_id=1, source_target_pairs={{0,16},{16,0},{32,48},{48,32},{64,80},{80,64},{96,112},{112,96},{1... | collective-permute-start | bytes 49160 | tf_op jit(solution)/shard_map/ppermute | solution.py:343
  43.7 1.0 collective-permute-done.5.far
  44.7 0.1 collective-permute-done.4.near
  44.9 1.8 %shard_map.97 = (bf16[16,168,128]{2,1,0:T(8,128)(2,1)}, bf16[2,128,128]{2,1,0:T(8,128)(2,1)S(1)}) custom-call(s32[1]{0:T(128)} %bitcast.core, bf16[64,128]{1,0:T(8,128)(2,1)S(1)} %get-tuple-element.26.own, bf16[64,128]{1,0:T(8,128)(2,1)S(1)} %collective-permute-done.4.near, bf16[64,128]{1,0:T(8,128)(2,1)S(1)} %collective-permute-done.5.far, ...), custom_call_target="tpu_custom_call" | custom-call | flops 250000000 | bytes 1048576 | tf_op jit(solution)/shard_map/pallas_call | solution.py:328
  46.7 3.7 %all-to-all-start.1 = ((bf16[16,168,128]{2,1,0:T(8,128)(2,1)}), bf16[16,168,128]{2,1,0:T(8,128)(2,1)S(1)}, u32[]{:S(2)}, u32[]{:S(2)}) async-start(bf16[16,168,128]{2,1,0:T(8,128)(2,1)} %get-tuple-element.32), calls=%async_computation.1 | async-start | bytes 1376256 | tf_op jit(solution)/shard_map/all_to_all | solution.py:356
  50.4 5.8 %collective-permute-start.7 = (bf16[128,128]{1,0:T(8,128)(2,1)S(1)}, bf16[128,128]{1,0:T(8,128)(2,1)S(1)}, u32[]{:S(2)}, u32[]{:S(2)}) collective-permute-start(bf16[128,128]{1,0:T(8,128)(2,1)S(1)} %get-tuple-element.48), channel_id=1, source_target_pairs={{16,32},{48,64},{80,96},{112,128},{144,160},{176,192},{208,224},{2... | collective-permute-start | bytes 98312 | tf_op jit(solution)/shard_map/ppermute | solution.py:348
  56.3 1.9 %collective-permute-start.6 = (bf16[128,128]{1,0:T(8,128)(2,1)S(1)}, bf16[128,128]{1,0:T(8,128)(2,1)S(1)}, u32[]{:S(2)}, u32[]{:S(2)}) collective-permute-start(bf16[128,128]{1,0:T(8,128)(2,1)S(1)} %get-tuple-element.49), channel_id=1, source_target_pairs={{0,16},{16,0},{32,48},{48,32},{64,80},{80,64},{96,112},{112,96},{1... | collective-permute-start | bytes 98312 | tf_op jit(solution)/shard_map/ppermute | solution.py:343
  58.2 1.2 collective-permute-done.6.near
  59.4 1.1 shard_map.98
  60.5 10.5 %all-to-all-done.1.parts = bf16[16,168,128]{2,1,0:T(8,128)(2,1)S(1)} async-done(((bf16[16,168,128]{2,1,0:T(8,128)(2,1)}), bf16[16,168,128]{2,1,0:T(8,128)(2,1)S(1)}, u32[]{:S(2)}, u32[]{:S(2)}) %all-to-all-start.1) | async-done | bytes 688160 | tf_op jit(solution)/shard_map/all_to_all | solution.py:356
  71.0 0.9 shard_map.99
  71.9 25.6 %all_to_all.25.terms = bf16[32,16,128]{2,1,0:T(8,128)(2,1)S(1)} all-to-all(bf16[32,16,128]{2,1,0:T(8,128)(2,1)S(1)} %get-tuple-element.38), channel_id=1, replica_groups=mesh['gz'=32,'grp'=16] {'gz'}, dimensions={0} | all-to-all | bytes 262144 | tf_op jit(solution)/shard_map/all_to_all | solution.py:356
  97.6 12.5 %all_to_all.26.terms = bf16[32,16,128]{2,1,0:T(8,128)(2,1)S(1)} all-to-all(bf16[32,16,128]{2,1,0:T(8,128)(2,1)S(1)} %shard_map.100), channel_id=1, replica_groups=mesh['gz'=32,'grp'=16] {'gz'}, dimensions={0} | all-to-all | bytes 262144 | tf_op jit(solution)/shard_map/all_to_all | solution.py:356
  110.1 0.7 shard_map.101
  110.8 17.1 %all_to_all.27 = bf16[16,88,128]{2,1,0:T(8,128)(2,1)S(1)} all-to-all(bf16[16,88,128]{2,1,0:T(8,128)(2,1)S(1)} %get-tuple-element.39), channel_id=1, replica_groups=mesh['gz'=32,'grp'=16] {'grp'}, dimensions={0} | all-to-all | bytes 720896 | tf_op jit(solution)/shard_map/all_to_all | solution.py:356
  127.9 0.9 shard_map.102
  (16 shorter events, 0.1 us)
Async XLA Ops:
  2.3 10.4 %copy-start.3 = (bf16[1,2,16,1024]{3,2,1,0:T(8,128)(2,1)S(1)}, bf16[1,2,16,1024]{3,2,1,0:T(8,128)(2,1)}, u32[]{:S(2)}) copy-start(bf16[1,2,16,1024]{3,2,1,0:T(8,128)(2,1)} %param.5) | copy-start | bytes 196612
  2.3 15.4 %copy-start.4 = (bf16[1728,64]{0,1:T(8,128)(2,1)S(1)}, bf16[1728,64]{0,1:T(8,128)(2,1)}, u32[]{:S(2)}) copy-start(bf16[1728,64]{0,1:T(8,128)(2,1)} %param.7) | copy-start | bytes 663556
  2.3 26.9 %all-to-all-start = ((bf16[16,8,1920]{2,1,0:T(8,128)(2,1)}), bf16[16,8,1920]{2,1,0:T(8,128)(2,1)S(1)}, u32[]{:S(2)}, u32[]{:S(2)}) async-start(bf16[16,8,1920]{2,1,0:T(8,128)(2,1)} %shard_map.94), calls=%async_computation | async-start | bytes 983040 | tf_op jit(solution)/shard_map/all_to_all | solution.py:356
  12.7 6.0 %collective-permute-start.1 = (bf16[16,1024]{1,0:T(8,128)(2,1)S(1)}, bf16[16,1024]{1,0:T(8,128)(2,1)S(1)}, u32[]{:S(2)}, u32[]{:S(2)}) collective-permute-start(bf16[16,1024]{1,0:T(8,128)(2,1)S(1)} %get-tuple-element.50), channel_id=1, source_target_pairs={{16,32},{48,64},{80,96},{112,128},{144,160},{176,192},{208,224},{2... | collective-permute-start | bytes 98312 | tf_op jit(solution)/shard_map/ppermute | solution.py:348
  15.7 3.1 %collective-permute-start = (bf16[16,1024]{1,0:T(8,128)(2,1)S(1)}, bf16[16,1024]{1,0:T(8,128)(2,1)S(1)}, u32[]{:S(2)}, u32[]{:S(2)}) collective-permute-start(bf16[16,1024]{1,0:T(8,128)(2,1)S(1)} %get-tuple-element.51), channel_id=1, source_target_pairs={{0,16},{16,0},{32,48},{48,32},{64,80},{80,64},{96,112},{112,96},{1... | collective-permute-start | bytes 98312 | tf_op jit(solution)/shard_map/ppermute | solution.py:343
  17.7 1.2 copy-start.1
  29.4 15.5 %copy-start = (bf16[4,128,256]{2,1,0:T(8,128)(2,1)S(1)}, bf16[4,128,256]{2,1,0:T(8,128)(2,1)}, u32[]{:S(2)}) copy-start(bf16[4,128,256]{2,1,0:T(8,128)(2,1)} %get-tuple-element.30.windows) | copy-start | bytes 786436
  29.4 15.5 %copy-start.2 = (f32[256,128]{1,0:T(8,128)S(1)}, f32[256,128]{1,0:T(8,128)}, u32[]{:S(2)}) copy-start(f32[256,128]{1,0:T(8,128)} %get-tuple-element.29.slope) | copy-start | bytes 393220
  29.4 9.4 %collective-permute-start.3 = (bf16[128,1920]{1,0:T(8,128)(2,1)S(1)}, bf16[128,1920]{1,0:T(8,128)(2,1)S(1)}, u32[]{:S(2)}, u32[]{:S(2)}) collective-permute-start(bf16[128,1920]{1,0:T(8,128)(2,1)S(1)} %shard_map.95.mine), channel_id=1, source_target_pairs={{0,16},{16,0},{32,48},{48,32},{64,80},{80,64},{96,112},{112,96},{1... | collective-permute-start | bytes 1474568 | tf_op jit(solution)/shard_map/ppermute | solution.py:343
  33.8 5.1 %collective-permute-start.2 = (bf16[64,128]{1,0:T(8,128)(2,1)S(1)}, bf16[64,128]{1,0:T(8,128)(2,1)S(1)}, u32[]{:S(2)}, u32[]{:S(2)}) collective-permute-start(bf16[64,128]{1,0:T(8,128)(2,1)S(1)} %get-tuple-element.25.coarse_in.own), channel_id=1, source_target_pairs={{16,32},{48,64},{80,96},{112,128},{144,160},{176,192},{208,224},{2... | collective-permute-start | bytes 49160 | tf_op jit(solution)/shard_map/ppermute | solution.py:348
  39.7 5.1 %collective-permute-start.5 = (bf16[64,128]{1,0:T(8,128)(2,1)S(1)}, bf16[64,128]{1,0:T(8,128)(2,1)S(1)}, u32[]{:S(2)}, u32[]{:S(2)}) collective-permute-start(bf16[64,128]{1,0:T(8,128)(2,1)S(1)} %get-tuple-element.26.own), channel_id=1, source_target_pairs={{16,32},{48,64},{80,96},{112,128},{144,160},{176,192},{208,224},{2... | collective-permute-start | bytes 49160 | tf_op jit(solution)/shard_map/ppermute | solution.py:348
  41.8 3.1 %collective-permute-start.4 = (bf16[64,128]{1,0:T(8,128)(2,1)S(1)}, bf16[64,128]{1,0:T(8,128)(2,1)S(1)}, u32[]{:S(2)}, u32[]{:S(2)}) collective-permute-start(bf16[64,128]{1,0:T(8,128)(2,1)S(1)} %get-tuple-element.26.own), channel_id=1, source_target_pairs={{0,16},{16,0},{32,48},{48,32},{64,80},{80,64},{96,112},{112,96},{1... | collective-permute-start | bytes 49160 | tf_op jit(solution)/shard_map/ppermute | solution.py:343
  46.7 12.7 %copy-start.5 = (bf16[9,256,128]{2,1,0:T(8,128)(2,1)S(1)}, bf16[9,256,128]{2,1,0:T(8,128)(2,1)}, u32[]{:S(2)}) copy-start(bf16[9,256,128]{2,1,0:T(8,128)(2,1)} %get-tuple-element.34.weights) | copy-start | bytes 1769476
  46.7 24.3 %all-to-all-start.1 = ((bf16[16,168,128]{2,1,0:T(8,128)(2,1)}), bf16[16,168,128]{2,1,0:T(8,128)(2,1)S(1)}, u32[]{:S(2)}, u32[]{:S(2)}) async-start(bf16[16,168,128]{2,1,0:T(8,128)(2,1)} %get-tuple-element.32), calls=%async_computation.1 | async-start | bytes 1376256 | tf_op jit(solution)/shard_map/all_to_all | solution.py:356
  50.4 7.8 %collective-permute-start.7 = (bf16[128,128]{1,0:T(8,128)(2,1)S(1)}, bf16[128,128]{1,0:T(8,128)(2,1)S(1)}, u32[]{:S(2)}, u32[]{:S(2)}) collective-permute-start(bf16[128,128]{1,0:T(8,128)(2,1)S(1)} %get-tuple-element.48), channel_id=1, source_target_pairs={{16,32},{48,64},{80,96},{112,128},{144,160},{176,192},{208,224},{2... | collective-permute-start | bytes 98312 | tf_op jit(solution)/shard_map/ppermute | solution.py:348
  56.3 3.1 %collective-permute-start.6 = (bf16[128,128]{1,0:T(8,128)(2,1)S(1)}, bf16[128,128]{1,0:T(8,128)(2,1)S(1)}, u32[]{:S(2)}, u32[]{:S(2)}) collective-permute-start(bf16[128,128]{1,0:T(8,128)(2,1)S(1)} %get-tuple-element.49), channel_id=1, source_target_pairs={{0,16},{16,0},{32,48},{48,32},{64,80},{80,64},{96,112},{112,96},{1... | collective-permute-start | bytes 98312 | tf_op jit(solution)/shard_map/ppermute | solution.py:343
